TPU v7x, 768 devices: a whole 4x8x12 slice. The times are simulated.
768 devices in a mesh: gx: 64 (over y, x, core), gy: 12 (over z).
Axes of the slice: x: 4, y: 8, z: 12, core: 2. Of those that a mesh axis runs over, the one named last changes fastest.
Arguments:
- right_side: float32 [1024, 768, 192], P('gx', 'gy'), may hold values from -46 to 46
- diagonal: float32 [1024, 768, 192], P('gx', 'gy'), may hold values from 0.1 to 2
Outputs:
- solution_field: float32 [1024, 768, 192], P('gx', 'gy')
- residual: float32 [1024, 768, 192], P('gx', 'gy')
All inputs are finite; a program needn't handle non-finite values.
Results may differ from a plain program's by a relative error of at most 0.00017.
Values sent between devices are 32-bit elements; how exact they have to be, the bound alone decides.
No kernel may reach another device: no remote copies, remote signals or barrier semaphores. Data moves between devices by JAX's collectives and lax.ppermute only.
A program may use at most 32 MiB of HBM per device.

v0:
```python
import jax
import jax.numpy as jnp
from jax import lax
from jax.sharding import Mesh
from jax.sharding import PartitionSpec as P

ITERS = 3
GX_GY = ("gx_0", "gx_1", "gx_2", "gy")
GX = ("gx_0", "gx_1", "gx_2")


def by_axis(x, axes):
    for axis in axes:
        x = lax.psum(x, axis)
    return x


def extended(block, sides, width):
    for axis, dim in sides:
        count = lax.axis_size(axis)
        forward = [(i, i + 1) for i in range(count - 1)]
        backward = [(target, source) for source, target in forward]
        low = lax.ppermute(
            lax.slice_in_dim(block, block.shape[dim] - width, None, axis=dim), axis, forward
        )
        high = lax.ppermute(lax.slice_in_dim(block, 0, width, axis=dim), axis, backward)
        block = jnp.concatenate([low, block, high], axis=dim)
    return block


def global_pair(residual, w_now):
    return (by_axis(jnp.sum(residual * residual), GX_GY), by_axis(jnp.sum(w_now * residual), GX_GY))


def trim_rim(field, layers):
    if layers == 0:
        return field
    return field[layers : field.shape[0] - layers, layers : field.shape[1] - layers]


def apply_local(field, diagonal, inside_mask):
    padded = jnp.pad(field, ((0, 0), (0, 0), (1, 1)))
    centre = padded[1:-1, 1:-1, 1:-1]
    beside = padded[2:, 1:-1, 1:-1] + padded[:-2, 1:-1, 1:-1]
    beside = beside + padded[1:-1, 2:, 1:-1] + padded[1:-1, :-2, 1:-1]
    beside = beside + padded[1:-1, 1:-1, 2:] + padded[1:-1, 1:-1, :-2]
    return inside_mask * ((6.0 + diagonal) * centre - beside)


def on_device(right_side, diagonal):
    solution_field = jnp.zeros_like(right_side)
    residual = right_side
    s_field = jnp.zeros_like(right_side)
    p_field = jnp.zeros_like(right_side)
    gamma_prev = jnp.float32(1.0)
    alpha_prev = jnp.float32(1.0)
    rim_depth = ITERS
    block_x = right_side.shape[0]
    block_y = right_side.shape[1]
    stacked = extended(jnp.stack((right_side, diagonal)), ((GX, 1), ("gy", 2)), rim_depth)
    source_pad = stacked[0]
    shift_pad = stacked[1]
    index_x = (
        lax.axis_index(GX) * block_x
        + jnp.arange(block_x + 2 * rim_depth, dtype=jnp.int32)
        - rim_depth
    )
    index_y = (
        lax.axis_index("gy") * block_y
        + jnp.arange(block_y + 2 * rim_depth, dtype=jnp.int32)
        - rim_depth
    )
    inside_x = (index_x >= 0) & (index_x < block_x * lax.axis_size(GX))
    inside_y = (index_y >= 0) & (index_y < block_y * lax.axis_size("gy"))
    inside_mask = (inside_x[:, None, None] & inside_y[None, :, None]).astype(jnp.float32)
    w_field = apply_local(source_pad, trim_rim(shift_pad, 1), trim_rim(inside_mask, 1))
    z_field = jnp.zeros_like(w_field)
    for step in range(ITERS):
        rim_now = rim_depth - 1 - step
        w_inner = trim_rim(w_field, rim_now)
        gamma, delta = global_pair(residual, w_inner)
        if step == 0:
            beta = jnp.float32(0.0)
            alpha = gamma / delta
        else:
            beta = gamma / gamma_prev
            alpha = gamma / (delta - beta * gamma / alpha_prev)
        s_field = w_inner + beta * s_field
        p_field = residual + beta * p_field
        solution_field = solution_field + alpha * p_field
        residual = residual - alpha * s_field
        if step + 1 < ITERS:
            layers = rim_depth - rim_now + 1
            q_field = apply_local(
                w_field, trim_rim(shift_pad, layers), trim_rim(inside_mask, layers)
            )
            z_field = q_field + beta * trim_rim(z_field, 1)
            w_field = trim_rim(w_field, 1) - alpha * z_field
        gamma_prev = gamma
        alpha_prev = alpha
    return (solution_field, residual)


def solution(mesh):
    torus = Mesh(mesh.devices.reshape(8, 4, 2, mesh.shape["gy"]), ("gx_0", "gx_1", "gx_2", "gy"))
    placed = (P(GX, "gy", None), P(GX, "gy", None))
    return jax.shard_map(
        on_device,
        mesh=torus,
        in_specs=placed,
        out_specs=(P(GX, "gy", None), P(GX, "gy", None)),
        check_vma=False,
    )
```

profile of v0, /device:TPU:10, one launch (start us, length us, event | category | flops | bytes accessed | tf_op | source)
XLA Modules:
  0.0 219.4 jit_solution(10135182575950386976)
XLA Ops:
  0.7 2.2 pad_maximum_fusion.2
  2.8 1.9 collective-permute-start
  4.7 3.6 %collective-permute-start.1 = (f32[2,3,64,192]{3,2,1,0:T(8,128)S(1)}, f32[2,3,64,192]{3,2,1,0:T(8,128)S(1)}, u32[]{:S(2)}, u32[]{:S(2)}) collective-permute-start(f32[2,3,64,192]{3,2,1,0:T(8,128)S(1)} %get-tuple-element.42), channel_id=1, source_target_pairs={{12,0},{24,12},{36,24},{48,36},{60,48},{72,60},{84,72},{96,84},{10... | collective-permute-start | bytes 884744 | tf_op jit(solution)/shard_map/ppermute | solution.py:26
  8.4 0.1 and_convert_fusion
  8.5 0.1 slice_bitcast_fusion.2
  8.7 3.5 %collective-permute-done = f32[2,3,64,192]{3,2,1,0:T(8,128)S(1)} collective-permute-done((f32[2,3,64,192]{3,2,1,0:T(8,128)}, f32[2,3,64,192]{3,2,1,0:T(8,128)S(1)}, u32[]{:S(2)}, u32[]{:S(2)}) %collective-permute-start) | collective-permute-done | bytes 294944 | tf_op jit(solution)/shard_map/ppermute | solution.py:23
  12.1 1.5 collective-permute-done.1
  13.7 4.3 %collective-permute-start.2 = (f32[2,22,3,192]{3,2,1,0:T(4,128)S(1)}, f32[2,22,3,192]{3,2,1,0:T(4,128)S(1)}, u32[]{:S(2)}, u32[]{:S(2)}) collective-permute-start(f32[2,22,3,192]{3,2,1,0:T(4,128)S(1)} %get-tuple-element.39), channel_id=1, source_target_pairs={{0,1},{1,2},{2,3},{3,4},{4,5},{5,6},{6,7},{7,8},{8,9},{9,10},{10,1... | collective-permute-start | bytes 304136 | tf_op jit(solution)/shard_map/ppermute | solution.py:23
  18.0 1.3 collective-permute-start.3
  19.3 0.1 slice_bitcast_fusion.4
  19.4 2.7 %collective-permute-done.2 = f32[2,22,3,192]{3,2,1,0:T(4,128)S(1)} collective-permute-done((f32[2,22,3,192]{3,2,1,0:T(4,128)S(1)}, f32[2,22,3,192]{3,2,1,0:T(4,128)S(1)}, u32[]{:S(2)}, u32[]{:S(2)}) %collective-permute-start.2) | collective-permute-done | bytes 101408 | tf_op jit(solution)/shard_map/ppermute | solution.py:23
  22.2 4.8 %collective-permute-done.3 = f32[2,22,3,192]{3,2,1,0:T(4,128)S(1)} collective-permute-done((f32[2,22,3,192]{3,2,1,0:T(4,128)S(1)}, f32[2,22,3,192]{3,2,1,0:T(4,128)S(1)}, u32[]{:S(2)}, u32[]{:S(2)}) %collective-permute-start.3) | collective-permute-done | bytes 101408 | tf_op jit(solution)/shard_map/ppermute | solution.py:26
  26.9 0.4 pad_maximum_fusion
  27.3 0.2 slice_bitcast_fusion.1
  27.6 1.8 fusion.3
  29.4 0.9 multiply_reduce_fusion.4
  30.3 16.8 %all-reduce.8 = (f32[]{:T(128)}, f32[]{:T(128)}) all-reduce(f32[]{:T(128)} %get-tuple-element.7, f32[]{:T(128)} %get-tuple-element.6), channel_id=1, replica_groups=mesh['gx_0'=8,'gx_1'=4,'gx_2'=2,'gy'=12] {'gx_0'}, use_global_device_ids=true, to_apply=%region_1.2 | all-reduce | flops 2 | bytes 16 | tf_op jit(solution)/shard_map/psum | solution.py:14
  47.1 10.5 %all-reduce.11 = (f32[]{:T(128)}, f32[]{:T(128)}) all-reduce(f32[]{:T(128)} %get-tuple-element.18, f32[]{:T(128)} %get-tuple-element.19), channel_id=1, replica_groups=mesh['gx_0'=8,'gx_1'=4,'gx_2'=2,'gy'=12] {'gx_1'}, use_global_device_ids=true, to_apply=%region_2.3 | all-reduce | flops 2 | bytes 16 | tf_op jit(solution)/shard_map/psum | solution.py:14
  57.6 3.1 %all-reduce.14 = (f32[]{:T(128)}, f32[]{:T(128)}) all-reduce(f32[]{:T(128)} %get-tuple-element.24, f32[]{:T(128)} %get-tuple-element.25), channel_id=1, replica_groups=mesh['gx_0'=8,'gx_1'=4,'gx_2'=2,'gy'=12] {'gx_2'}, use_global_device_ids=true, to_apply=%region_3.4 | all-reduce | flops 2 | bytes 16 | tf_op jit(solution)/shard_map/psum | solution.py:14
  60.7 30.8 %all-reduce.5 = (f32[]{:T(128)}, f32[]{:T(128)}) all-reduce(f32[]{:T(128)} %get-tuple-element.30, f32[]{:T(128)} %get-tuple-element.31), channel_id=1, replica_groups=mesh['gx_0'=8,'gx_1'=4,'gx_2'=2,'gy'=12] {'gy'}, use_global_device_ids=true, to_apply=%region_4.5 | all-reduce | flops 2 | bytes 16 | tf_op jit(solution)/shard_map/psum | solution.py:14
  92.8 3.7 %multiply_subtract_fusion = (f32[18,66,192]{2,1,0:T(8,128)S(1)}, f32[18,66,192]{2,1,0:T(8,128)}) fusion(f32[20,68,192]{2,1,0:T(8,128)S(1)} %fusion.3, f32[]{:T(128)S(6)} %div.21, f32[22,70,192]{2,1,0:T(8,128)} %copy-done.2, f32[18,66]{1,0:T(8,128)S(1)} %slice_bitcast_fusion.2), kind=kLoop, calls=%fused_computation.25 | loop fusion | flops 2509056 | bytes 10859524 | tf_op jit(solution)/shard_map/sub | solution.py:98
  96.5 2.0 multiply_reduce_fusion.2
  98.5 16.3 %all-reduce.7 = (f32[]{:T(128)}, f32[]{:T(128)}) all-reduce(f32[]{:T(128)} %get-tuple-element.5, f32[]{:T(128)} %get-tuple-element.4), channel_id=1, replica_groups=mesh['gx_0'=8,'gx_1'=4,'gx_2'=2,'gy'=12] {'gx_0'}, use_global_device_ids=true, to_apply=%region_11.12 | all-reduce | flops 2 | bytes 16 | tf_op jit(solution)/shard_map/psum | solution.py:14
  114.8 8.9 %all-reduce.10 = (f32[]{:T(128)}, f32[]{:T(128)}) all-reduce(f32[]{:T(128)} %get-tuple-element.16, f32[]{:T(128)} %get-tuple-element.17), channel_id=1, replica_groups=mesh['gx_0'=8,'gx_1'=4,'gx_2'=2,'gy'=12] {'gx_1'}, use_global_device_ids=true, to_apply=%region_12.13 | all-reduce | flops 2 | bytes 16 | tf_op jit(solution)/shard_map/psum | solution.py:14
  123.7 3.1 %all-reduce.13 = (f32[]{:T(128)}, f32[]{:T(128)}) all-reduce(f32[]{:T(128)} %get-tuple-element.22, f32[]{:T(128)} %get-tuple-element.23), channel_id=1, replica_groups=mesh['gx_0'=8,'gx_1'=4,'gx_2'=2,'gy'=12] {'gx_2'}, use_global_device_ids=true, to_apply=%region_13.14 | all-reduce | flops 2 | bytes 16 | tf_op jit(solution)/shard_map/psum | solution.py:14
  126.8 22.4 %all-reduce.4 = (f32[]{:T(128)}, f32[]{:T(128)}) all-reduce(f32[]{:T(128)} %get-tuple-element.28, f32[]{:T(128)} %get-tuple-element.29), channel_id=1, replica_groups=mesh['gx_0'=8,'gx_1'=4,'gx_2'=2,'gy'=12] {'gy'}, use_global_device_ids=true, to_apply=%region_14.15 | all-reduce | flops 2 | bytes 16 | tf_op jit(solution)/shard_map/psum | solution.py:14
  153.4 5.0 %multiply_reduce_fusion = (f32[]{:T(128)}, f32[]{:T(128)}, f32[16,64,192]{2,1,0:T(8,128)}, f32[16,64,192]{2,1,0:T(8,128)}) fusion(f32[18,66,192]{2,1,0:T(8,128)} %get-tuple-element.36, f32[]{:T(128)S(6)} %div.22, f32[18,66,192]{2,1,0:T(8,128)S(1)} %get-tuple-element.35, f32[22,70,192]{2,1,0:T(8,128)} %copy-done.2, f32[16,64]{1,0:T(8,128)S(1)} %slice_bitcast_fusion.4, ...), kind=kLoop, calls=%fused_computation.43 | loop fusion | flops 4128766 | bytes 11558928 | tf_op jit(solution)/shard_map/reduce_sum | solution.py:32
  158.4 16.1 %all-reduce.6 = (f32[]{:T(128)}, f32[]{:T(128)}) all-reduce(f32[]{:T(128)} %get-tuple-element.3, f32[]{:T(128)} %get-tuple-element.2), channel_id=1, replica_groups=mesh['gx_0'=8,'gx_1'=4,'gx_2'=2,'gy'=12] {'gx_0'}, use_global_device_ids=true, to_apply=%region_21.22 | all-reduce | flops 2 | bytes 16 | tf_op jit(solution)/shard_map/psum | solution.py:14
  174.5 10.4 %all-reduce.9 = (f32[]{:T(128)}, f32[]{:T(128)}) all-reduce(f32[]{:T(128)} %get-tuple-element.14, f32[]{:T(128)} %get-tuple-element.15), channel_id=1, replica_groups=mesh['gx_0'=8,'gx_1'=4,'gx_2'=2,'gy'=12] {'gx_1'}, use_global_device_ids=true, to_apply=%region_22.23 | all-reduce | flops 2 | bytes 16 | tf_op jit(solution)/shard_map/psum | solution.py:14
  184.9 3.2 %all-reduce.12 = (f32[]{:T(128)}, f32[]{:T(128)}) all-reduce(f32[]{:T(128)} %get-tuple-element.20, f32[]{:T(128)} %get-tuple-element.21), channel_id=1, replica_groups=mesh['gx_0'=8,'gx_1'=4,'gx_2'=2,'gy'=12] {'gx_2'}, use_global_device_ids=true, to_apply=%region_23.24 | all-reduce | flops 2 | bytes 16 | tf_op jit(solution)/shard_map/psum | solution.py:14
  188.1 23.3 %all-reduce.3 = (f32[]{:T(128)}, f32[]{:T(128)}) all-reduce(f32[]{:T(128)} %get-tuple-element.26, f32[]{:T(128)} %get-tuple-element.27), channel_id=1, replica_groups=mesh['gx_0'=8,'gx_1'=4,'gx_2'=2,'gy'=12] {'gy'}, use_global_device_ids=true, to_apply=%region_24.25 | all-reduce | flops 2 | bytes 16 | tf_op jit(solution)/shard_map/psum | solution.py:14
  215.2 4.3 %multiply_subtract_fusion.1 = (f32[16,64,192]{2,1,0:T(8,128)}, f32[16,64,192]{2,1,0:T(8,128)}) fusion(f32[16,64,192]{2,1,0:T(8,128)} %get-tuple-element.33, f32[16,64,192]{2,1,0:T(8,128)} %get-tuple-element.32, f32[]{:T(128)S(6)} %div.25, f32[]{:T(128)S(6)} %div.27, f32[20,68,192]{2,1,0:T(8,128)S(1)} %fusion.3, f32[]{:T(128)S(6)} %div.22, ...), kind=kLoop, calls=%fused_computation.41 | loop fusion | flops 2949120 | bytes 6291476 | tf_op jit(solution)/shard_map/sub | solution.py:91
  (12 shorter events, 0.2 us)
Async XLA Ops:
  0.6 13.0 %copy-start = (f32[16,64,192]{2,1,0:T(8,128)S(1)}, f32[16,64,192]{2,1,0:T(8,128)}, u32[]{:S(2)}) copy-start(f32[16,64,192]{2,1,0:T(8,128)} %param.2) | copy-start | bytes 2359300
  0.6 13.0 %copy-start.3 = (f32[16,64,192]{2,1,0:T(8,128)S(1)}, f32[16,64,192]{2,1,0:T(8,128)}, u32[]{:S(2)}) copy-start(f32[16,64,192]{2,1,0:T(8,128)} %param.3) | copy-start | bytes 2359300
  2.8 9.3 %collective-permute-start = (f32[2,3,64,192]{3,2,1,0:T(8,128)}, f32[2,3,64,192]{3,2,1,0:T(8,128)S(1)}, u32[]{:S(2)}, u32[]{:S(2)}) collective-permute-start(f32[2,3,64,192]{3,2,1,0:T(8,128)} %get-tuple-element.41), channel_id=1, source_target_pairs={{0,12},{12,24},{24,36},{36,48},{48,60},{60,72},{72,84},{84,96},{96... | collective-permute-start | bytes 884744 | tf_op jit(solution)/shard_map/ppermute | solution.py:23
  4.7 8.9 %collective-permute-start.1 = (f32[2,3,64,192]{3,2,1,0:T(8,128)S(1)}, f32[2,3,64,192]{3,2,1,0:T(8,128)S(1)}, u32[]{:S(2)}, u32[]{:S(2)}) collective-permute-start(f32[2,3,64,192]{3,2,1,0:T(8,128)S(1)} %get-tuple-element.42), channel_id=1, source_target_pairs={{12,0},{24,12},{36,24},{48,36},{60,48},{72,60},{84,72},{96,84},{10... | collective-permute-start | bytes 884744 | tf_op jit(solution)/shard_map/ppermute | solution.py:26
  13.7 8.4 %collective-permute-start.2 = (f32[2,22,3,192]{3,2,1,0:T(4,128)S(1)}, f32[2,22,3,192]{3,2,1,0:T(4,128)S(1)}, u32[]{:S(2)}, u32[]{:S(2)}) collective-permute-start(f32[2,22,3,192]{3,2,1,0:T(4,128)S(1)} %get-tuple-element.39), channel_id=1, source_target_pairs={{0,1},{1,2},{2,3},{3,4},{4,5},{5,6},{6,7},{7,8},{8,9},{9,10},{10,1... | collective-permute-start | bytes 304136 | tf_op jit(solution)/shard_map/ppermute | solution.py:23
  18.0 8.9 %collective-permute-start.3 = (f32[2,22,3,192]{3,2,1,0:T(4,128)S(1)}, f32[2,22,3,192]{3,2,1,0:T(4,128)S(1)}, u32[]{:S(2)}, u32[]{:S(2)}) collective-permute-start(f32[2,22,3,192]{3,2,1,0:T(4,128)S(1)} %get-tuple-element.40), channel_id=1, source_target_pairs={{1,0},{2,1},{3,2},{4,3},{5,4},{6,5},{7,6},{8,7},{9,8},{10,9},{11,1... | collective-permute-start | bytes 304136 | tf_op jit(solution)/shard_map/ppermute | solution.py:26
  27.6 1.8 copy-start.2
  92.7 3.7 %copy-start.1 = (f32[16,64,192]{2,1,0:T(8,128)S(1)}, f32[16,64,192]{2,1,0:T(8,128)}, u32[]{:S(2)}) copy-start(f32[16,64,192]{2,1,0:T(8,128)} %param.2) | copy-start | bytes 2359300
where the time goes:
time: 220 us; the launch traced here: 219 us
  blocking collectives  165 us (75%)
  other arithmetic  20.4 us (9%)
  waiting for transfers between devices  12.5 us (6%)
  starting transfers between devices  11.1 us (5%)
  between operations  10 us (5%)
    psum x12, blocking collectives, by_axis(): x = lax.psum(x, axis)  165 us
    reduce_sum x3, other arithmetic, global_pair(): jnp.sum(w_now * residual)  7.92 us
    ppermute x2, waiting for transfers between devices, extended(): lax.ppermute(lax.slice_in_dim(block, 0, width, axis=dim), axis, backward)  6.3 us
    ppermute x2, waiting for transfers between devices, extended(): lax.ppermute(lax.slice_in_dim(block, block.shape[dim] - width, None, axis...  6.2 us
    ppermute x2, starting transfers between devices, extended(): lax.ppermute(lax.slice_in_dim(block, block.shape[dim] - width, None, axis...  6.19 us
    ppermute x2, starting transfers between devices, extended(): lax.ppermute(lax.slice_in_dim(block, 0, width, axis=dim), axis, backward)  4.93 us
  transfers between devices with their start and end apart: 4, of which 4 were waited for; matrix products, arithmetic and copies ran while one was open for 0% of the time, Pallas kernels for 0%

commit v1 on v0

v1 whole, which is shorter than its diff:
```python
import jax
import jax.numpy as jnp
from jax import lax
from jax.experimental import pallas as pl
from jax.experimental.pallas import tpu as pltpu
from jax.sharding import Mesh
from jax.sharding import PartitionSpec as P


SHIFT = 7.0
GRAIN = 8.0
GX = ("y", "x", "c")
FIRST = ("y", "c")
SECOND = ("x", "z")
F32 = jnp.float32
DEPTH = 3


def two_sum(a, b):
    s = a + b
    t = s - a
    return s, (a - (s - t)) + (b - t)


def halves(a):
    t = a * 4097.0
    high = t - (t - a)
    return high, a - high


def scaled(pair, factor):
    high, low = halves(pair[0])
    s, e = two_sum(high * factor, low * factor)
    return s, e + pair[1] * factor


def added(one, two):
    s, e = two_sum(one[0], two[0])
    return two_sum(s, e + (one[1] + two[1]))


def translated(moments, step):
    row = list(moments)
    out = [row[0]]
    while len(row) > 1:
        row = [added(row[k + 1], scaled(row[k], step)) for k in range(len(row) - 1)]
        out.append(row[0])
    return out


def to_grain(x):
    return jnp.floor(x * GRAIN + 0.5) / GRAIN


def iota(shape, dim):
    return lax.broadcasted_iota(jnp.int32, shape, dim)


def pack_y(b, d, forward, backward):
    nx, ny, nz = b.shape
    sub = iota((nx, 8, nz), 1)
    last = d[:, ny - 8 : ny, :]
    forward[...] = jnp.where(sub >= 5, b[:, ny - 8 : ny, :], pltpu.roll(last, 4, 1))
    backward[...] = jnp.where(sub < 3, b[:, 0:8, :], pltpu.roll(d[:, 0:8, :], 4, 1))


def rims(low, high):
    sub = iota(low.shape, low.ndim - 2)
    field = jnp.where(sub >= 5, low, jnp.where(sub < 3, high, 0.0))
    low_shift = pltpu.roll(low, 4, low.ndim - 2)
    high_shift = pltpu.roll(high, 4, low.ndim - 2)
    shift = jnp.where(sub >= 6, low_shift, jnp.where(sub < 2, high_shift, 0.0))
    return field, shift


def pack_x(b, d, ylow, yhigh, forward, backward):
    nx, ny, nz = b.shape
    for out, bx, dx in ((forward, nx - 3, nx - 2), (backward, 0, 0)):
        out[0:3, 0:ny, :] = b[bx : bx + 3, :, :]
        out[3:5, 0:ny, :] = d[dx : dx + 2, :, :]
        field, _ = rims(ylow[bx : bx + 3], yhigh[bx : bx + 3])
        _, shift = rims(ylow[dx : dx + 2], yhigh[dx : dx + 2])
        out[0:3, ny : ny + 8, :] = field
        out[3:5, ny : ny + 8, :] = shift


def wide(a):
    nz = a.shape[-1]
    return jnp.pad(a, ((0, 0),) * (a.ndim - 1) + ((0, 256 - nz),))


def fields(edge, b, d, ylow, yhigh, xlow, xhigh, u1, u2, u3, row_out, c_out, u0, dx, keep):
    nx, ny, nz = b.shape
    rows = ny + 16

    def place(into, at, own, rim):
        sub = iota((8, 256), 0)
        rim = wide(rim)
        into[at, 8 : 8 + ny, :] = wide(own)
        into[at, 0:8, :] = jnp.where(sub >= 5, rim, 0.0)
        into[at, 8 + ny : rows, :] = jnp.where(sub < 3, rim, 0.0)

    def own(i, carry):
        field, shift = rims(ylow[i], yhigh[i])
        place(u0, i + 3, b[i], field)
        place(dx, i + 2, d[i], shift)
        return carry

    lax.fori_loop(0, nx, own, 0)
    for j in range(3):
        place(u0, j, xlow[j, 0:ny], xlow[j, ny : ny + 8])
        place(u0, nx + 3 + j, xhigh[j, 0:ny], xhigh[j, ny : ny + 8])
    for j in range(2):
        place(dx, j, xlow[3 + j, 0:ny], xlow[3 + j, ny : ny + 8])
        place(dx, nx + 2 + j, xhigh[3 + j, 0:ny], xhigh[3 + j, ny : ny + 8])
    at_row = iota((rows, 256), 0)
    side = jnp.where(at_row < 8, edge[2], jnp.where(at_row >= 8 + ny, edge[3], 1.0))
    keep[...] = jnp.where(iota((rows, 256), 1) < nz, side, 0.0)

    def applied(field, at, shift_at, base):
        mid = field[at]
        beside = field[at - 1] + field[at + 1]
        beside = beside + (pltpu.roll(mid, 1, 0) + pltpu.roll(mid, rows - 1, 0))
        beside = beside + (pltpu.roll(mid, 1, 1) + pltpu.roll(mid, 255, 1))
        return (dx[shift_at] + base) * mid - beside

    def folded(a):
        return jnp.sum(a[8 : 8 + ny].reshape(ny // 8, 8, 256), axis=0)

    def total(a):
        return jnp.sum(a, axis=(0, 1), keepdims=True)

    def probe(i, carry):
        mid = u0[4 * i + 3] * keep[...]
        return carry[0] + folded(mid * mid), carry[1] + folded(mid * applied(u0, 4 * i + 3, 4 * i + 2, 6.0))

    zero = jnp.zeros((8, 256), F32)
    norm, lift = lax.fori_loop(0, nx // 4, probe, (zero, zero))
    norm = total(norm)
    lift = total(lift)
    shift = jnp.where(norm > 0.0, lift / jnp.where(norm > 0.0, norm, 1.0), SHIFT)
    shift = to_grain(jnp.clip(shift, 0.0, 14.0))
    base = 6.0 - shift

    def along(i, count):
        return jnp.where(i < count, edge[0], jnp.where(i >= nx + count, edge[1], 1.0))

    def first(i, carry):
        u1[i] = applied(u0, i + 1, i, base) * (keep[...] * along(i, 2))
        return carry

    def second(i, carry):
        u2[i] = applied(u1, i + 1, i + 1, base) * (keep[...] * along(i, 1))
        return carry

    def third(i, carry):
        new = applied(u2, i + 1, i + 2, base) * keep[...]
        u3[i] = new[8 : 8 + ny]
        f0 = u0[i + 3]
        f1 = u1[i + 2]
        f2 = u2[i + 1]
        return (
            carry[0] + folded(f0 * f0),
            carry[1] + folded(f0 * f1),
            carry[2] + folded(f1 * f1),
            carry[3] + folded(f1 * f2),
            carry[4] + folded(f2 * f2),
            carry[5] + folded(f2 * new),
        )

    lax.fori_loop(0, nx + 4, first, 0)
    lax.fori_loop(0, nx + 2, second, 0)
    sums = lax.fori_loop(0, nx, third, (zero,) * 6)
    sums = [jnp.broadcast_to(total(a), (8, 128)) for a in sums]
    step = jnp.broadcast_to(shift, (8, 128)) - SHIFT
    pairs = translated([(a, jnp.zeros((8, 128), F32)) for a in sums], step)
    lane = iota((8, 128), 1)
    line = jnp.zeros((8, 128), F32)
    for k, (high, low) in enumerate(pairs):
        line = jnp.where(lane == k, high, jnp.where(lane == k + 6, low, line))
    for k in range(row_out.shape[0] // 8):
        row_out[8 * k : 8 * k + 8, :] = line
    c_out[...] = jnp.broadcast_to(shift, (8, 128))


def gathered(rows):
    parts = [(rows[8 * k : 8 * k + 8], jnp.zeros((8, 128), F32)) for k in range(rows.shape[0] // 8)]

    def joined(one, two):
        s, e = two_sum(one[0], two[0])
        return s, e + (one[1] + two[1])

    while len(parts) > 1:
        parts = [joined(*parts[k : k + 2]) if k + 1 < len(parts) else parts[k] for k in range(0, len(parts), 2)]
    s, e = parts[0]
    for by in (4, 2, 1):
        s, e = joined((s, e), (pltpu.roll(s, by, 0), pltpu.roll(e, by, 0)))
    lane = iota((8, 128), 1)
    return jnp.where(lane < 6, s, s + pltpu.roll(e, 6, 1))


def regroup(rows, out):
    line = gathered(rows)
    for k in range(out.shape[0] // 8):
        out[8 * k : 8 * k + 8, :] = line


def steps_of(moments, centre):
    def form(one, two):
        out = 0.0
        for k in range(len(one) + len(two) - 1):
            part = 0.0
            for i in range(len(one)):
                if 0 <= k - i < len(two):
                    part = part + one[i] * two[k - i]
            out = out + part * moments[k]
        return out

    def plus(one, factor, two):
        size = max(len(one), len(two))
        out = []
        for k in range(size):
            if k >= len(two):
                out.append(one[k])
            elif k >= len(one):
                out.append(factor * two[k])
            else:
                out.append(one[k] + factor * two[k])
        return out

    unit = jnp.ones_like(moments[0])
    residual = [unit]
    solution_field = []
    s = []
    p = []
    for step in range(3):
        raised = [residual[0] * centre]
        for k in range(1, len(residual)):
            raised.append(residual[k - 1] + centre * residual[k])
        raised.append(residual[-1])
        gamma = form(residual, residual)
        delta = form(residual, raised)
        if step == 0:
            alpha = gamma / delta
            s, p = raised, residual
        else:
            beta = gamma / gamma_prev
            alpha = gamma / (delta - beta * gamma / alpha_prev)
            s = plus(raised, beta, s)
            p = plus(residual, beta, p)
        solution_field = plus(solution_field, alpha, p)
        residual = plus(residual, -alpha, s)
        gamma_prev = gamma
        alpha_prev = alpha
    return solution_field, residual


def recentred(coefficients, step):
    out = list(coefficients)
    size = len(out)
    for i in range(size - 1):
        for k in range(size - 2, i - 1, -1):
            out[k] = out[k] + step * out[k + 1]
    return out


def finish(rows, c_in, b, u1, u2, u3, solution_field, residual, coef):
    nz = b.shape[2]
    i = pl.program_id(0)
    block = b.shape[0]

    @pl.when(i == 0)
    def _():
        line = gathered(rows)
        lane = lambda k: jnp.broadcast_to(jnp.sum(jnp.where(iota((8, 128), 1) == k, line, 0.0), axis=1, keepdims=True), (8, 128))
        moments = [(lane(k), lane(k + 6)) for k in range(6)]
        away = to_grain(moments[1][0] / moments[0][0])
        moments = [high + low for high, low in translated(moments, -away)]
        centre = SHIFT + away
        xs, rs = steps_of(moments, centre)
        step = c_in[...] - centre
        xs = recentred(xs, step)
        rs = recentred(rs, step)
        for k, value in enumerate(xs + rs):
            coef[k] = value

    def coefficient(k):
        return coef[k, 0:1, 0:1]

    for j in range(block):
        at = i * block + j
        f0 = b[j]
        f1 = u1[at + 2, 8:-8, 0:nz]
        f2 = u2[at + 1, 8:-8, 0:nz]
        f3 = u3[at, :, 0:nz]
        solution_field[j] = coefficient(0) * f0 + coefficient(1) * f1 + coefficient(2) * f2
        residual[j] = coefficient(3) * f0 + coefficient(4) * f1 + coefficient(5) * f2 + coefficient(6) * f3


def shifted(a, axis, by):
    count = lax.axis_size(axis)
    pairs = [(k, k + by) for k in range(count) if 0 <= k + by < count]
    return lax.ppermute(a, axis, pairs)


def spread(rows, axes):
    count = lax.axis_size(axes)
    out = lax.all_to_all(rows[:count].reshape(count, 1, 128), axes, 0, 0, tiled=True)
    return jnp.pad(out.reshape(count, 128), ((0, -count % 8), (0, 0)))


VMEM = pl.BlockSpec(memory_space=pltpu.VMEM)
SMEM = pl.BlockSpec(memory_space=pltpu.SMEM)


def call(body, out_shapes, count, scratch=(), smem=0, name=None):
    return pl.pallas_call(
        body,
        out_shape=out_shapes,
        in_specs=[SMEM] * smem + [VMEM] * (count - smem),
        out_specs=[VMEM] * len(out_shapes),
        scratch_shapes=list(scratch),
        name=name,
    )


def on_device(right_side, diagonal):
    nx, ny, nz = right_side.shape
    rows = ny + 16
    shape = lambda *dims: jax.ShapeDtypeStruct(dims, F32)
    yf, yb = call(pack_y, (shape(nx, 8, nz),) * 2, 2, name="pack_y")(right_side, diagonal)
    ylow = shifted(yf, "z", 1)
    yhigh = shifted(yb, "z", -1)
    xf, xb = call(pack_x, (shape(5, ny + 8, nz),) * 2, 4, name="pack_x")(right_side, diagonal, ylow, yhigh)
    xlow = shifted(xf, GX, 1)
    xhigh = shifted(xb, GX, -1)
    gx = lax.axis_index(GX)
    gy = lax.axis_index("z")
    edge = jnp.stack(
        [gx > 0, gx < lax.axis_size(GX) - 1, gy > 0, gy < lax.axis_size("z") - 1]
    ).astype(F32)
    up = lambda n: -(-n // 8) * 8
    one = lax.axis_size(FIRST)
    two = lax.axis_size(SECOND)
    u1, u2, u3, line, shift = call(
        fields,
        (shape(nx + 4, rows, 256), shape(nx + 2, rows, 256), shape(nx, ny, 256), shape(up(one), 128), shape(8, 128)),
        7,
        scratch=(pltpu.VMEM((nx + 6, rows, 256), F32), pltpu.VMEM((nx + 4, rows, 256), F32), pltpu.VMEM((rows, 256), F32)),
        smem=1,
        name="fields",
    )(edge, right_side, diagonal, ylow, yhigh, xlow, xhigh)
    line = spread(line, FIRST)
    (line,) = call(regroup, (shape(up(two), 128),), 1, name="regroup")(line)
    line = spread(line, SECOND)
    block = 2
    tile = pl.BlockSpec((block, ny, nz), lambda i: (i, 0, 0))
    return pl.pallas_call(
        finish,
        out_shape=(shape(nx, ny, nz),) * 2,
        grid=(nx // block,),
        in_specs=[VMEM, VMEM, tile, VMEM, VMEM, VMEM],
        out_specs=[tile, tile],
        scratch_shapes=[pltpu.VMEM((7, 8, 128), F32)],
        name="finish",
    )(line, shift, right_side, u1, u2, u3)


def solution_on(mesh, split):
    torus = Mesh(mesh.devices.reshape(*split, mesh.shape["gy"]), GX + ("z",))
    placed = (P(GX, "z", None), P(GX, "z", None))
    return jax.shard_map(on_device, mesh=torus, in_specs=placed, out_specs=placed, check_vma=False)


def solution(mesh):
    return solution_on(mesh, (8, 4, 2))
```

time: 220 us -> 97.5 us (0.44)
  the two profiles are of different devices: /device:TPU:10 before, /device:TPU:1 now
where the time goes in v1:
time: 97.5 us; the launch traced here: 97 us
  blocking collectives  45.2 us (46%)
  Pallas kernels  24.2 us (25%)
  starting transfers between devices  16.8 us (17%)
  waiting for transfers between devices  8.03 us (8%)
  local copies, waits for them, and re-layouts  1.4 us (1%)
    all_to_all x2, blocking collectives, spread(): lax.all_to_all(rows[:count].reshape(count, 1, 128), axes, 0, 0, tiled=True)  45.2 us
    ppermute x4, starting transfers between devices, shifted(): return lax.ppermute(a, axis, pairs)  16.8 us
    pallas_call x1, Pallas kernels, on_device(): call(fields, (shape(nx + 4, rows, 256), shape(nx + 2, rows, 256), shape(n...  10.8 us
    ppermute x4, waiting for transfers between devices, shifted(): return lax.ppermute(a, axis, pairs)  8.03 us
    pallas_call x1, Pallas kernels, on_device(): pl.pallas_call(finish, out_shape=(shape(nx, ny, nz),) * 2, grid=(nx // bl...  7.3 us
    pallas_call x1, Pallas kernels, on_device(): call(pack_x, (shape(5, ny + 8, nz),) * 2, 4, name='pack_x')  2.46 us
    pallas_call x1, Pallas kernels, on_device(): call(pack_y, (shape(nx, 8, nz),) * 2, 2, name='pack_y')  2.26 us
  transfers between devices with their start and end apart: 4, of which 3 were waited for; matrix products, arithmetic and copies ran while one was open for 1% of the time, Pallas kernels for 0%

profile of v1, /device:TPU:1, one launch (start us, length us, event | category | flops | bytes accessed | tf_op | source)
XLA Modules:
  0.0 97.0 jit_solution(18339060225813507679)
XLA Ops:
  0.6 2.3 %pack_y.1 = (f32[16,8,192]{2,1,0:T(8,128)}, f32[16,8,192]{2,1,0:T(8,128)}) custom-call(f32[16,64,192]{2,1,0:T(8,128)} %b.7, f32[16,64,192]{2,1,0:T(8,128)} %d.5), custom_call_target="tpu_custom_call" | custom-call | tf_op jit(solution)/shard_map/pack_y/pallas_call | solution.py:331
  2.9 4.8 %collective-permute-start = (f32[16,8,192]{2,1,0:T(8,128)}, f32[16,8,192]{2,1,0:T(8,128)S(1)}, u32[]{:S(2)}, u32[]{:S(2)}) collective-permute-start(f32[16,8,192]{2,1,0:T(8,128)} %get-tuple-element.11), channel_id=1, source_target_pairs={{0,1},{1,2},{2,3},{3,4},{4,5},{5,6},{6,7},{7,8},{8,9},{9,10},{10,1... | collective-permute-start | bytes 294920 | tf_op jit(solution)/shard_map/ppermute | solution.py:303
  7.7 1.3 %collective-permute-start.1 = (f32[16,8,192]{2,1,0:T(8,128)}, f32[16,8,192]{2,1,0:T(8,128)S(1)}, u32[]{:S(2)}, u32[]{:S(2)}) collective-permute-start(f32[16,8,192]{2,1,0:T(8,128)} %get-tuple-element.12), channel_id=1, source_target_pairs={{1,0},{2,1},{3,2},{4,3},{5,4},{6,5},{7,6},{8,7},{9,8},{10,9},{11,1... | collective-permute-start | bytes 294920 | tf_op jit(solution)/shard_map/ppermute | solution.py:303
  9.0 0.9 collective-permute-done.ylow
  9.9 0.0 copy-start
  9.9 4.3 %collective-permute-done.1.yhigh = f32[16,8,192]{2,1,0:T(8,128)S(1)} collective-permute-done((f32[16,8,192]{2,1,0:T(8,128)}, f32[16,8,192]{2,1,0:T(8,128)S(1)}, u32[]{:S(2)}, u32[]{:S(2)}) %collective-permute-start.1) | collective-permute-done | bytes 98336 | tf_op jit(solution)/shard_map/ppermute | solution.py:303
  14.3 0.0 copy-done
  14.3 0.0 copy-start.1
  14.3 0.7 copy-done.1
  14.9 2.5 %pack_x.1 = (f32[5,72,192]{2,1,0:T(8,128)}, f32[5,72,192]{2,1,0:T(8,128)}) custom-call(f32[16,64,192]{2,1,0:T(8,128)} %b.7, f32[16,64,192]{2,1,0:T(8,128)} %d.5, f32[16,8,192]{2,1,0:T(8,128)} %copy-done, f32[16,8,192]{2,1,0:T(8,128)} %copy-done.1), custom_call_target="tpu_custom_call" | custom-call | tf_op jit(solution)/shard_map/pack_x/pallas_call | solution.py:334
  17.4 5.1 %collective-permute-start.2 = (f32[5,72,192]{2,1,0:T(8,128)}, f32[5,72,192]{2,1,0:T(8,128)S(1)}, u32[]{:S(2)}, u32[]{:S(2)}) collective-permute-start(f32[5,72,192]{2,1,0:T(8,128)} %get-tuple-element.13), channel_id=1, source_target_pairs={{0,12},{12,24},{24,36},{36,48},{48,60},{60,72},{72,84},{84,96},{96... | collective-permute-start | bytes 829448 | tf_op jit(solution)/shard_map/ppermute | solution.py:303
  22.5 5.6 %collective-permute-start.3 = (f32[5,72,192]{2,1,0:T(8,128)}, f32[5,72,192]{2,1,0:T(8,128)S(1)}, u32[]{:S(2)}, u32[]{:S(2)}) collective-permute-start(f32[5,72,192]{2,1,0:T(8,128)} %get-tuple-element.14), channel_id=1, source_target_pairs={{12,0},{24,12},{36,24},{48,36},{60,48},{72,60},{84,72},{96,84},{10... | collective-permute-start | bytes 829448 | tf_op jit(solution)/shard_map/ppermute | solution.py:303
  28.1 0.6 add_convert_fusion.edge
  28.7 0.0 collective-permute-done.2.xlow
  28.7 0.0 copy-start.2
  28.8 2.8 %collective-permute-done.3.xhigh = f32[5,72,192]{2,1,0:T(8,128)S(1)} collective-permute-done((f32[5,72,192]{2,1,0:T(8,128)}, f32[5,72,192]{2,1,0:T(8,128)S(1)}, u32[]{:S(2)}, u32[]{:S(2)}) %collective-permute-start.3) | collective-permute-done | bytes 276512 | tf_op jit(solution)/shard_map/ppermute | solution.py:303
  31.5 0.0 copy-done.2
  31.5 0.0 copy-start.3
  31.5 0.7 copy-done.3
  32.3 10.8 %fields.1 = (f32[20,80,256]{2,1,0:T(8,128)}, f32[18,80,256]{2,1,0:T(8,128)}, f32[16,64,256]{2,1,0:T(8,128)}, f32[16,128]{1,0:T(8,128)}, f32[8,128]{1,0:T(8,128)}) custom-call(f32[4]{0:T(128)} %add_convert_fusion.edge, f32[16,64,192]{2,1,0:T(8,128)} %b.7, f32[16,64,192]{2,1,0:T(8,128)} %d.5, f32[16,8,192]{2,1,0:T(8,128)} %copy-done, f32[16,8,192]{2,1,0:T(8,128)} %copy-done.1, ...), custom_call_target="tpu_custom_call" | custom-call | tf_op jit(solution)/shard_map/fields/pallas_call | solution.py:345
  43.1 16.4 %all_to_all.10 = f32[16,1,128]{2,1,0:T(1,128)} all-to-all(f32[16,1,128]{2,1,0:T(1,128)} %bitcast.15), channel_id=1, replica_groups=mesh['y'=8,'x'=4,'c'=2,'z'=12] {'y','c'}, dimensions={0} | all-to-all | bytes 16384 | tf_op jit(solution)/shard_map/all_to_all | solution.py:308
  59.5 1.4 %regroup.1 = f32[48,128]{1,0:T(8,128)} custom-call(f32[16,128]{1,0:T(8,128)} %bitcast.14), custom_call_target="tpu_custom_call" | custom-call | tf_op jit(solution)/shard_map/regroup/pallas_call | solution.py:354
  60.9 28.7 %all_to_all.11 = f32[48,1,128]{2,1,0:T(1,128)} all-to-all(f32[48,1,128]{2,1,0:T(1,128)} %bitcast.13), channel_id=1, replica_groups=mesh['y'=8,'x'=4,'c'=2,'z'=12] {'x','z'}, dimensions={0} | all-to-all | bytes 49152 | tf_op jit(solution)/shard_map/all_to_all | solution.py:308
  89.7 7.3 %finish.1 = (f32[16,64,192]{2,1,0:T(8,128)}, f32[16,64,192]{2,1,0:T(8,128)}) custom-call(f32[48,128]{1,0:T(8,128)} %bitcast.12, f32[8,128]{1,0:T(8,128)} %get-tuple-element.16.c_in, f32[16,64,192]{2,1,0:T(8,128)} %b.7, f32[20,80,256]{2,1,0:T(8,128)} %get-tuple-element.17.u1, f32[18,80,256]{2,1,0:T(8,128)} %get-tuple-element.18.u2, ...), custom_call_target="tpu_custom_call" | custom-call | tf_op jit(solution)/shard_map/finish/pallas_call | solution.py:358
Async XLA Ops:
  2.9 7.1 %collective-permute-start = (f32[16,8,192]{2,1,0:T(8,128)}, f32[16,8,192]{2,1,0:T(8,128)S(1)}, u32[]{:S(2)}, u32[]{:S(2)}) collective-permute-start(f32[16,8,192]{2,1,0:T(8,128)} %get-tuple-element.11), channel_id=1, source_target_pairs={{0,1},{1,2},{2,3},{3,4},{4,5},{5,6},{6,7},{7,8},{8,9},{9,10},{10,1... | collective-permute-start | bytes 294920 | tf_op jit(solution)/shard_map/ppermute | solution.py:303
  7.7 6.6 %collective-permute-start.1 = (f32[16,8,192]{2,1,0:T(8,128)}, f32[16,8,192]{2,1,0:T(8,128)S(1)}, u32[]{:S(2)}, u32[]{:S(2)}) collective-permute-start(f32[16,8,192]{2,1,0:T(8,128)} %get-tuple-element.12), channel_id=1, source_target_pairs={{1,0},{2,1},{3,2},{4,3},{5,4},{6,5},{7,6},{8,7},{9,8},{10,9},{11,1... | collective-permute-start | bytes 294920 | tf_op jit(solution)/shard_map/ppermute | solution.py:303
  9.9 4.3 %copy-start = (f32[16,8,192]{2,1,0:T(8,128)}, f32[16,8,192]{2,1,0:T(8,128)S(1)}, u32[]{:S(2)}) copy-start(f32[16,8,192]{2,1,0:T(8,128)S(1)} %collective-permute-done.ylow) | copy-start | bytes 294916
  14.3 0.7 copy-start.1
  17.4 11.4 %collective-permute-start.2 = (f32[5,72,192]{2,1,0:T(8,128)}, f32[5,72,192]{2,1,0:T(8,128)S(1)}, u32[]{:S(2)}, u32[]{:S(2)}) collective-permute-start(f32[5,72,192]{2,1,0:T(8,128)} %get-tuple-element.13), channel_id=1, source_target_pairs={{0,12},{12,24},{24,36},{36,48},{48,60},{60,72},{72,84},{84,96},{96... | collective-permute-start | bytes 829448 | tf_op jit(solution)/shard_map/ppermute | solution.py:303
  22.5 9.0 %collective-permute-start.3 = (f32[5,72,192]{2,1,0:T(8,128)}, f32[5,72,192]{2,1,0:T(8,128)S(1)}, u32[]{:S(2)}, u32[]{:S(2)}) collective-permute-start(f32[5,72,192]{2,1,0:T(8,128)} %get-tuple-element.14), channel_id=1, source_target_pairs={{12,0},{24,12},{36,24},{48,36},{60,48},{72,60},{84,72},{96,84},{10... | collective-permute-start | bytes 829448 | tf_op jit(solution)/shard_map/ppermute | solution.py:303
  28.7 2.8 %copy-start.2 = (f32[5,72,192]{2,1,0:T(8,128)}, f32[5,72,192]{2,1,0:T(8,128)S(1)}, u32[]{:S(2)}) copy-start(f32[5,72,192]{2,1,0:T(8,128)S(1)} %collective-permute-done.2.xlow) | copy-start | bytes 829444
  31.5 0.7 copy-start.3

commit v2 on v1

--- a/solution.py
+++ b/solution.py
@@ -13,7 +13,7 @@
 FIRST = ("y", "c")
 SECOND = ("x", "z")
 F32 = jnp.float32
-DEPTH = 3
+GRANT = 24 << 20
 
 
 def two_sum(a, b):
@@ -320,6 +320,7 @@
         in_specs=[SMEM] * smem + [VMEM] * (count - smem),
         out_specs=[VMEM] * len(out_shapes),
         scratch_shapes=list(scratch),
+        compiler_params=pltpu.CompilerParams(vmem_limit_bytes=GRANT),
         name=name,
     )
 
@@ -327,7 +328,7 @@
 def on_device(right_side, diagonal):
     nx, ny, nz = right_side.shape
     rows = ny + 16
-    shape = lambda *dims: jax.ShapeDtypeStruct(dims, F32)
+    shape = lambda *dims: pltpu.VMEM(dims, F32)
     yf, yb = call(pack_y, (shape(nx, 8, nz),) * 2, 2, name="pack_y")(right_side, diagonal)
     ylow = shifted(yf, "z", 1)
     yhigh = shifted(yb, "z", -1)
@@ -357,11 +358,12 @@
     tile = pl.BlockSpec((block, ny, nz), lambda i: (i, 0, 0))
     return pl.pallas_call(
         finish,
-        out_shape=(shape(nx, ny, nz),) * 2,
+        out_shape=(jax.ShapeDtypeStruct((nx, ny, nz), F32),) * 2,
         grid=(nx // block,),
         in_specs=[VMEM, VMEM, tile, VMEM, VMEM, VMEM],
         out_specs=[tile, tile],
         scratch_shapes=[pltpu.VMEM((7, 8, 128), F32)],
+        compiler_params=pltpu.CompilerParams(vmem_limit_bytes=GRANT),
         name="finish",
     )(line, shift, right_side, u1, u2, u3)
 

time: 97.5 us -> 85.7 us (0.88)
  Pallas kernels: 24.2 us -> 12.3 us
  local copies, waits for them, and re-layouts: 1.4 us -> 2.46 us
    pallas_call x1, Pallas kernels: 7.3 us -> 3.5 us  [on_device(): pl.pallas_call(finish, out_shape=(jax.ShapeDtypeStruct((nx, ny, nz), F32)...]
    pallas_call x1, Pallas kernels: 10.8 us -> 7.84 us  [on_device(): call(fields, (shape(nx + 4, rows, 256), shape(nx + 2, rows, 256), shape(n...]
    pallas_call x1, Pallas kernels: 2.26 us -> 0.03 us  [on_device(): call(pack_y, (shape(nx, 8, nz),) * 2, 2, name='pack_y')]
    pallas_call x1, Pallas kernels: 2.46 us -> 0.79 us  [on_device(): call(pack_x, (shape(5, ny + 8, nz),) * 2, 4, name='pack_x')]
    pallas_call x1, Pallas kernels: 1.39 us -> 0.09 us  [on_device(): line, = call(regroup, (shape(up(two), 128),), 1, name='regroup')(line)]
    unnamed x8, local copies, waits for them, and re-layouts: 1.4 us -> 2.46 us
  transfers between devices with their start and end apart: 4 -> 4, of which waited for: 3 -> 3; matrix products, arithmetic and copies ran while one was open for 1% -> 0% of each run, Pallas kernels for 0% -> 0%
where the time goes in v2:
time: 85.7 us; the launch traced here: 85.4 us
  blocking collectives  44.7 us (52%)
  starting transfers between devices  16.9 us (20%)
  Pallas kernels  12.3 us (14%)
  waiting for transfers between devices  8.18 us (10%)
  local copies, waits for them, and re-layouts  2.46 us (3%)
    all_to_all x2, blocking collectives, spread(): lax.all_to_all(rows[:count].reshape(count, 1, 128), axes, 0, 0, tiled=True)  44.7 us
    ppermute x4, starting transfers between devices, shifted(): return lax.ppermute(a, axis, pairs)  16.9 us
    ppermute x4, waiting for transfers between devices, shifted(): return lax.ppermute(a, axis, pairs)  8.18 us
    pallas_call x1, Pallas kernels, on_device(): call(fields, (shape(nx + 4, rows, 256), shape(nx + 2, rows, 256), shape(n...  7.84 us
    pallas_call x1, Pallas kernels, on_device(): pl.pallas_call(finish, out_shape=(jax.ShapeDtypeStruct((nx, ny, nz), F32)...  3.5 us
    unnamed x8, local copies, waits for them, and re-layouts  2.46 us
  transfers between devices with their start and end apart: 4, of which 3 were waited for; matrix products, arithmetic and copies ran while one was open for 0% of the time, Pallas kernels for 0%

profile of v2, /device:TPU:1, one launch (start us, length us, event | category | flops | bytes accessed | tf_op | source)
XLA Modules:
  0.0 85.4 jit_solution(5276670005530290822)
XLA Ops:
  0.6 0.0 copy-start
  0.6 1.2 %copy-done = f32[16,64,192]{2,1,0:T(8,128)S(1)} copy-done((f32[16,64,192]{2,1,0:T(8,128)S(1)}, f32[16,64,192]{2,1,0:T(8,128)}, u32[]{:S(2)}) %copy-start) | copy-done | bytes 786456
  1.9 0.0 copy-start.2
  1.9 1.2 %copy-done.2 = f32[16,64,192]{2,1,0:T(8,128)S(1)} copy-done((f32[16,64,192]{2,1,0:T(8,128)S(1)}, f32[16,64,192]{2,1,0:T(8,128)}, u32[]{:S(2)}) %copy-start.2) | copy-done | bytes 786456
  3.1 0.0 copy-start.1
  3.1 0.0 copy-start.3
  3.1 5.0 %collective-permute-start = (f32[16,8,192]{2,1,0:T(8,128)S(1)}, f32[16,8,192]{2,1,0:T(8,128)S(1)}, u32[]{:S(2)}, u32[]{:S(2)}) collective-permute-start(f32[16,8,192]{2,1,0:T(8,128)S(1)} %get-tuple-element.11), channel_id=1, source_target_pairs={{0,1},{1,2},{2,3},{3,4},{4,5},{5,6},{6,7},{7,8},{8,9},{9,10},{10,1... | collective-permute-start | bytes 294920 | tf_op jit(solution)/shard_map/ppermute | solution.py:303
  8.1 1.3 %collective-permute-start.1 = (f32[16,8,192]{2,1,0:T(8,128)S(1)}, f32[16,8,192]{2,1,0:T(8,128)S(1)}, u32[]{:S(2)}, u32[]{:S(2)}) collective-permute-start(f32[16,8,192]{2,1,0:T(8,128)S(1)} %get-tuple-element.12), channel_id=1, source_target_pairs={{1,0},{2,1},{3,2},{4,3},{5,4},{6,5},{7,6},{8,7},{9,8},{10,9},{11,1... | collective-permute-start | bytes 294920 | tf_op jit(solution)/shard_map/ppermute | solution.py:303
  9.4 0.6 collective-permute-done.ylow
  10.0 4.4 %collective-permute-done.1.yhigh = f32[16,8,192]{2,1,0:T(8,128)S(1)} collective-permute-done((f32[16,8,192]{2,1,0:T(8,128)S(1)}, f32[16,8,192]{2,1,0:T(8,128)S(1)}, u32[]{:S(2)}, u32[]{:S(2)}) %collective-permute-start.1) | collective-permute-done | bytes 98336 | tf_op jit(solution)/shard_map/ppermute | solution.py:303
  14.5 0.8 pack_x.1
  15.2 5.1 %collective-permute-start.2 = (f32[5,72,192]{2,1,0:T(8,128)}, f32[5,72,192]{2,1,0:T(8,128)S(1)}, u32[]{:S(2)}, u32[]{:S(2)}) collective-permute-start(f32[5,72,192]{2,1,0:T(8,128)} %get-tuple-element.13), channel_id=1, source_target_pairs={{0,12},{12,24},{24,36},{36,48},{48,60},{60,72},{72,84},{84,96},{96... | collective-permute-start | bytes 829448 | tf_op jit(solution)/shard_map/ppermute | solution.py:303
  20.3 5.6 %collective-permute-start.3 = (f32[5,72,192]{2,1,0:T(8,128)S(1)}, f32[5,72,192]{2,1,0:T(8,128)S(1)}, u32[]{:S(2)}, u32[]{:S(2)}) collective-permute-start(f32[5,72,192]{2,1,0:T(8,128)S(1)} %get-tuple-element.14), channel_id=1, source_target_pairs={{12,0},{24,12},{36,24},{48,36},{60,48},{72,60},{84,72},{96,84},{10... | collective-permute-start | bytes 829448 | tf_op jit(solution)/shard_map/ppermute | solution.py:303
  26.0 0.1 add_convert_fusion.edge
  26.0 0.0 collective-permute-done.2.xlow
  26.0 3.1 %collective-permute-done.3.xhigh = f32[5,72,192]{2,1,0:T(8,128)S(1)} collective-permute-done((f32[5,72,192]{2,1,0:T(8,128)S(1)}, f32[5,72,192]{2,1,0:T(8,128)S(1)}, u32[]{:S(2)}, u32[]{:S(2)}) %collective-permute-start.3) | collective-permute-done | bytes 276512 | tf_op jit(solution)/shard_map/ppermute | solution.py:303
  29.2 0.0 copy-done.1
  29.2 0.0 copy-done.3
  29.2 7.8 %fields.1 = (f32[20,80,256]{2,1,0:T(8,128)S(1)}, f32[18,80,256]{2,1,0:T(8,128)S(1)}, f32[16,64,256]{2,1,0:T(8,128)S(1)}, f32[16,128]{1,0:T(8,128)S(1)}, f32[8,128]{1,0:T(8,128)S(1)}) custom-call(f32[4]{0:T(128)S(1)} %add_convert_fusion.edge, f32[16,64,192]{2,1,0:T(8,128)S(1)} %copy-done.1, f32[16,64,192]{2,1,0:T(8,128)S(1)} %copy-done.3, ...), custom_call_target="tpu_custom_call" | custom-call | tf_op jit(solution)/shard_map/fields/pallas_call | solution.py:346
  37.0 16.0 %all_to_all.10 = f32[16,1,128]{2,1,0:T(1,128)S(1)} all-to-all(f32[16,1,128]{2,1,0:T(1,128)S(1)} %bitcast.15), channel_id=1, replica_groups=mesh['y'=8,'x'=4,'c'=2,'z'=12] {'y','c'}, dimensions={0} | all-to-all | bytes 16384 | tf_op jit(solution)/shard_map/all_to_all | solution.py:308
  53.0 0.1 regroup.1
  53.1 28.7 %all_to_all.11 = f32[48,1,128]{2,1,0:T(1,128)S(1)} all-to-all(f32[48,1,128]{2,1,0:T(1,128)S(1)} %bitcast.13), channel_id=1, replica_groups=mesh['y'=8,'x'=4,'c'=2,'z'=12] {'x','z'}, dimensions={0} | all-to-all | bytes 49152 | tf_op jit(solution)/shard_map/all_to_all | solution.py:308
  81.8 3.5 %finish.1 = (f32[16,64,192]{2,1,0:T(8,128)}, f32[16,64,192]{2,1,0:T(8,128)}) custom-call(f32[48,128]{1,0:T(8,128)S(1)} %bitcast.12, f32[8,128]{1,0:T(8,128)S(1)} %get-tuple-element.16.c_in, f32[16,64,192]{2,1,0:T(8,128)S(1)} %copy-done.1, f32[20,80,256]{2,1,0:T(8,128)S(1)} %get-tuple-element.17.u1, f32[18,80,256]{2,1,0:T(8,128)S(1)} %get-tuple-element.18.u2, ...), custom_call_target="tpu_custom_call" | custom-call | tf_op jit(solution)/shard_map/finish/pallas_call | solution.py:359
  (1 shorter events, 0.0 us)
Async XLA Ops:
  0.6 1.2 %copy-start = (f32[16,64,192]{2,1,0:T(8,128)S(1)}, f32[16,64,192]{2,1,0:T(8,128)}, u32[]{:S(2)}) copy-start(f32[16,64,192]{2,1,0:T(8,128)} %b.7) | copy-start | bytes 2359300
  1.9 1.2 %copy-start.2 = (f32[16,64,192]{2,1,0:T(8,128)S(1)}, f32[16,64,192]{2,1,0:T(8,128)}, u32[]{:S(2)}) copy-start(f32[16,64,192]{2,1,0:T(8,128)} %d.5) | copy-start | bytes 2359300
  3.1 26.0 %copy-start.1 = (f32[16,64,192]{2,1,0:T(8,128)S(1)}, f32[16,64,192]{2,1,0:T(8,128)}, u32[]{:S(2)}) copy-start(f32[16,64,192]{2,1,0:T(8,128)} %b.7) | copy-start | bytes 2359300
  3.1 26.0 %copy-start.3 = (f32[16,64,192]{2,1,0:T(8,128)S(1)}, f32[16,64,192]{2,1,0:T(8,128)}, u32[]{:S(2)}) copy-start(f32[16,64,192]{2,1,0:T(8,128)} %d.5) | copy-start | bytes 2359300
  3.1 6.9 %collective-permute-start = (f32[16,8,192]{2,1,0:T(8,128)S(1)}, f32[16,8,192]{2,1,0:T(8,128)S(1)}, u32[]{:S(2)}, u32[]{:S(2)}) collective-permute-start(f32[16,8,192]{2,1,0:T(8,128)S(1)} %get-tuple-element.11), channel_id=1, source_target_pairs={{0,1},{1,2},{2,3},{3,4},{4,5},{5,6},{6,7},{7,8},{8,9},{9,10},{10,1... | collective-permute-start | bytes 294920 | tf_op jit(solution)/shard_map/ppermute | solution.py:303
  8.1 6.3 %collective-permute-start.1 = (f32[16,8,192]{2,1,0:T(8,128)S(1)}, f32[16,8,192]{2,1,0:T(8,128)S(1)}, u32[]{:S(2)}, u32[]{:S(2)}) collective-permute-start(f32[16,8,192]{2,1,0:T(8,128)S(1)} %get-tuple-element.12), channel_id=1, source_target_pairs={{1,0},{2,1},{3,2},{4,3},{5,4},{6,5},{7,6},{8,7},{9,8},{10,9},{11,1... | collective-permute-start | bytes 294920 | tf_op jit(solution)/shard_map/ppermute | solution.py:303
  15.2 10.8 %collective-permute-start.2 = (f32[5,72,192]{2,1,0:T(8,128)}, f32[5,72,192]{2,1,0:T(8,128)S(1)}, u32[]{:S(2)}, u32[]{:S(2)}) collective-permute-start(f32[5,72,192]{2,1,0:T(8,128)} %get-tuple-element.13), channel_id=1, source_target_pairs={{0,12},{12,24},{24,36},{36,48},{48,60},{60,72},{72,84},{84,96},{96... | collective-permute-start | bytes 829448 | tf_op jit(solution)/shard_map/ppermute | solution.py:303
  20.3 8.8 %collective-permute-start.3 = (f32[5,72,192]{2,1,0:T(8,128)S(1)}, f32[5,72,192]{2,1,0:T(8,128)S(1)}, u32[]{:S(2)}, u32[]{:S(2)}) collective-permute-start(f32[5,72,192]{2,1,0:T(8,128)S(1)} %get-tuple-element.14), channel_id=1, source_target_pairs={{12,0},{24,12},{36,24},{48,36},{60,48},{72,60},{84,72},{96,84},{10... | collective-permute-start | bytes 829448 | tf_op jit(solution)/shard_map/ppermute | solution.py:303

commit v3 on v2

v3 whole, which is shorter than its diff:
```python
import jax
import jax.numpy as jnp
from jax import lax
from jax.experimental import pallas as pl
from jax.experimental.pallas import tpu as pltpu
from jax.sharding import Mesh
from jax.sharding import PartitionSpec as P


SHIFT = 7.0
GRAIN = 8.0
GX = ("y", "x", "c")
FIRST = ("y", "c")
SECOND = ("x", "z")
F32 = jnp.float32
GRANT = 24 << 20
PARTS = 4


def two_sum(a, b):
    s = a + b
    t = s - a
    return s, (a - (s - t)) + (b - t)


def halves(a):
    t = a * 4097.0
    high = t - (t - a)
    return high, a - high


def scaled(pair, factor):
    high, low = halves(pair[0])
    s, e = two_sum(high * factor, low * factor)
    return s, e + pair[1] * factor


def added(one, two):
    s, e = two_sum(one[0], two[0])
    return two_sum(s, e + (one[1] + two[1]))


def translated(moments, step):
    row = list(moments)
    out = [row[0]]
    while len(row) > 1:
        row = [added(row[k + 1], scaled(row[k], step)) for k in range(len(row) - 1)]
        out.append(row[0])
    return out


def to_grain(x):
    return jnp.floor(x * GRAIN + 0.5) / GRAIN


def iota(shape, dim):
    return lax.broadcasted_iota(jnp.int32, shape, dim)


def place():
    gx = lax.axis_index(GX)
    gy = lax.axis_index("z")
    is_there = lambda x: x.astype(jnp.int32)
    return (
        lax.axis_index("c"),
        is_there(gx > 0),
        is_there(gx < lax.axis_size(GX) - 1),
        is_there(gy > 0),
        is_there(gy < lax.axis_size("z") - 1),
    )


def half_turn(a):
    return pltpu.roll(a, 64, a.ndim - 1)


def squeeze(first, second):
    left = lax.broadcasted_iota(jnp.int32, first.shape, first.ndim - 1) < 64
    return jnp.where(left, first, half_turn(second))


def lanes(block):
    rest = jnp.pad(block[..., 128:], ((0, 0),) * (block.ndim - 1) + ((0, 64),))
    return block[..., :128], rest


def pack(b, d, u0, dx, yf, yb, off, on, sems):
    where = place()
    nx, ny, _ = b.shape
    copies = [
        pltpu.make_async_copy(source, target.at[3 : 3 + nx, 8 : 8 + ny, :], sems.at[k])
        for k, (source, target) in enumerate(((b, u0), (d, dx)))
    ]
    for copy in copies:
        copy.start()
    for copy in copies:
        copy.wait()
    half = nx // 2

    def y_face(row, first_row):
        field = u0[3 : 3 + nx, row : row + 8, :]
        shift = pltpu.roll(dx[3 : 3 + nx, row : row + 8, :], 4, 1)
        sub = iota(field.shape, 1)
        face = jnp.where(sub < 3 if first_row else sub >= 5, field, shift)
        main, rest = lanes(face)
        return main, squeeze(rest[:half], rest[half:])

    for out, row, first_row in ((yf, ny, False), (yb, 8, True)):
        main, rest = y_face(row, first_row)
        out[0:nx] = main
        out[nx : nx + half] = rest
    mid = ny // 2
    for out, high in ((off, where[0]), (on, 1 - where[0])):
        for j in range(5):
            if j < 3:
                slab = u0[3 + j + high * (nx - 3), 8 : 8 + ny, :]
            else:
                slab = dx[j + high * (nx - 2), 8 : 8 + ny, :]
            main, rest = lanes(slab)
            out[j, 0:ny, :] = main
            out[j, ny : ny + mid, :] = squeeze(rest[:mid], rest[mid:])


def unsqueeze(main, rest, second):
    rest = half_turn(rest) if second else rest
    return jnp.concatenate([main, rest[..., :64]], axis=-1)


def corners(u0_in, dx_in, ylow, yhigh, u0, dx, off, on):
    where = place()
    nx = u0.shape[0] - 6
    ny = u0.shape[1] - 16
    half = nx // 2
    for halo, row in ((ylow, 0), (yhigh, 8 + ny)):
        for k in (0, 1):
            part = slice(k * half, (k + 1) * half)
            tile = unsqueeze(halo[part], halo[nx : nx + half], k == 1)
            at = slice(3 + k * half, 3 + (k + 1) * half)
            u0[at, row : row + 8, :] = tile
            dx[at, row : row + 8, :] = pltpu.roll(tile, 4, 1)
    for out, high in ((off, where[0]), (on, 1 - where[0])):
        one = 3 + high * (nx - 1)
        two = 4 + high * (nx - 3)
        for j, (field, at) in enumerate(((u0, one), (u0, two), (dx, one))):
            low = field[at, 0:8, :]
            out[j] = jnp.where(iota(low.shape, 0) >= 4, low, field[at, 8 + ny : 16 + ny, :])


def stencil(field, dx, at, base):
    mid = field[at]
    rows = mid.shape[0]
    padded = jnp.pad(mid, ((0, 0), (0, 256 - mid.shape[1])))
    beside = field[at - 1] + field[at + 1]
    beside = beside + (pltpu.roll(mid, 1, 0) + pltpu.roll(mid, rows - 1, 0))
    across = pltpu.roll(padded, 1, 1) + pltpu.roll(padded, 255, 1)
    return (dx[at] + base) * mid - (beside + across[:, : mid.shape[1]])


def fold(a):
    rows = a.shape[0] - 16
    return jnp.sum(a[8 : 8 + rows].reshape(rows // 8, 8, a.shape[1]), axis=0)


def total(a):
    return jnp.broadcast_to(jnp.sum(a, axis=(0, 1), keepdims=True), (8, 128))


def side_mask(where, shape):
    rows = iota(shape, 0)
    low = jnp.full(shape, where[3].astype(F32))
    high = jnp.full(shape, where[4].astype(F32))
    return jnp.where(rows < 8, low, jnp.where(rows >= shape[0] - 8, high, 1.0))


def products(f0, f1, f2, f3):
    return tuple(fold(p) for p in (f0 * f0, f0 * f1, f1 * f1, f1 * f2, f2 * f2)) + (
        jnp.sum((f2[8:-8] * f3).reshape(-1, 8, f3.shape[1]), axis=0),
    )


def accumulated(sums, more):
    return tuple(a + b for a, b in zip(sums, more))


def middle(u0, dx, u1, u2, u3, sums_out, shift_out, keep):
    where = place()
    nx = u0.shape[0] - 6
    shape = u0.shape[1:]
    zero = jnp.zeros((8, shape[1]), F32)
    keep[...] = side_mask(where, shape)

    def probe(i, carry):
        at = 5 + 3 * i
        mid = u0[at]
        return carry[0] + fold(mid * mid), carry[1] + fold(mid * stencil(u0, dx, at, 6.0))

    norm, lift = lax.fori_loop(0, 4, probe, (zero, zero), unroll=2)
    norm = total(norm)
    lift = total(lift)
    shift = jnp.where(norm > 0.0, lift / jnp.where(norm > 0.0, norm, 1.0), SHIFT)
    shift = to_grain(jnp.clip(shift, 0.0, 14.0))
    shift_out[...] = shift
    base = 6.0 - shift[0:1, 0:1]

    def first(i, carry):
        u1[i] = stencil(u0, dx, i, base) * keep[...]
        return carry

    def second(i, carry):
        u2[i] = stencil(u1, dx, i, base) * keep[...]
        return carry

    def third(i, sums):
        new = stencil(u2, dx, i, base)[8:-8]
        u3[i - 3] = new
        return accumulated(sums, products(u0[i], u1[i], u2[i], new))

    lax.fori_loop(4, nx + 2, first, 0, unroll=2)
    lax.fori_loop(5, nx + 1, second, 0, unroll=2)
    sums = lax.fori_loop(6, nx, third, (zero,) * 6)
    for k in range(6):
        sums_out[k] = sums[k]


def rim(u0_in, dx_in, u1_in, u2_in, u3_in, sums_in, shift_in, off, on, coff, con, u0, dx, u1, u2, u3, row_out):
    where = place()
    nx = u0.shape[0] - 6
    ny = u0.shape[1] - 16
    mid = ny // 2
    shape = u0.shape[1:]
    for main, corner, high in ((off, coff, where[0]), (on, con, 1 - where[0])):
        for j in range(5):
            slab = main[j, 0:ny, :]
            rest = main[j, ny : ny + mid, :]
            top = unsqueeze(slab[:mid], rest, False)
            bottom = unsqueeze(slab[mid:], rest, True)
            field, at = (u0, j + high * (nx + 3)) if j < 3 else (dx, j - 2 + high * (nx + 2))
            field[at, 8 : 8 + mid, :] = top
            field[at, 8 + mid : 8 + ny, :] = bottom
        one = 2 + high * (nx + 1)
        two = 1 + high * (nx + 3)
        for j, (field, at) in enumerate(((u0, one), (u0, two), (dx, one))):
            tile = corner[j]
            field[at, 0:8, :] = tile
            field[at, 8 + ny : 16 + ny, :] = tile
    keep = side_mask(where, shape)
    shift = shift_in[...]
    base = 6.0 - shift[0:1, 0:1]
    low = where[1].astype(F32)
    high = where[2].astype(F32)

    def first(i, carry):
        u1[1 + i] = stencil(u0, dx, 1 + i, base) * (keep * jnp.where(i < 2, low, 1.0))
        u1[nx + 2 + i] = stencil(u0, dx, nx + 2 + i, base) * (keep * jnp.where(i > 0, high, 1.0))
        return carry

    def second(i, carry):
        u2[2 + i] = stencil(u1, dx, 2 + i, base) * (keep * jnp.where(i < 1, low, 1.0))
        u2[nx + 1 + i] = stencil(u1, dx, nx + 1 + i, base) * (keep * jnp.where(i > 1, high, 1.0))
        return carry

    def third(i, sums):
        for at in (3 + i, nx + i):
            new = stencil(u2, dx, at, base)[8:-8]
            u3[at - 3] = new
            sums = accumulated(sums, products(u0[at], u1[at], u2[at], new))
        return sums

    lax.fori_loop(0, 3, first, 0)
    lax.fori_loop(0, 3, second, 0)
    sums = lax.fori_loop(0, 3, third, tuple(sums_in[k] for k in range(6)))
    pairs = translated([(total(a), jnp.zeros((8, 128), F32)) for a in sums], shift - SHIFT)
    lane = iota((8, 128), 1)
    line = jnp.zeros((8, 128), F32)
    for k, (high_part, low_part) in enumerate(pairs):
        line = jnp.where(lane == k, high_part, jnp.where(lane == k + 6, low_part, line))
    for k in range(row_out.shape[0] // 8):
        row_out[8 * k : 8 * k + 8, :] = line


def gathered(rows):
    parts = [(rows[8 * k : 8 * k + 8], jnp.zeros((8, 128), F32)) for k in range(rows.shape[0] // 8)]

    def joined(one, two):
        s, e = two_sum(one[0], two[0])
        return s, e + (one[1] + two[1])

    while len(parts) > 1:
        parts = [joined(*parts[k : k + 2]) if k + 1 < len(parts) else parts[k] for k in range(0, len(parts), 2)]
    s, e = parts[0]
    for by in (4, 2, 1):
        s, e = joined((s, e), (pltpu.roll(s, by, 0), pltpu.roll(e, by, 0)))
    lane = iota((8, 128), 1)
    return jnp.where(lane < 6, s, s + pltpu.roll(e, 6, 1))


def regroup(rows, out):
    line = gathered(rows)
    for k in range(out.shape[0] // 8):
        out[8 * k : 8 * k + 8, :] = line


def steps_of(moments, centre):
    def form(one, two):
        out = 0.0
        for k in range(len(one) + len(two) - 1):
            part = 0.0
            for i in range(len(one)):
                if 0 <= k - i < len(two):
                    part = part + one[i] * two[k - i]
            out = out + part * moments[k]
        return out

    def plus(one, factor, two):
        size = max(len(one), len(two))
        out = []
        for k in range(size):
            if k >= len(two):
                out.append(one[k])
            elif k >= len(one):
                out.append(factor * two[k])
            else:
                out.append(one[k] + factor * two[k])
        return out

    unit = jnp.ones_like(moments[0])
    residual = [unit]
    solution_field = []
    s = []
    p = []
    for step in range(3):
        raised = [residual[0] * centre]
        for k in range(1, len(residual)):
            raised.append(residual[k - 1] + centre * residual[k])
        raised.append(residual[-1])
        gamma = form(residual, residual)
        delta = form(residual, raised)
        if step == 0:
            alpha = gamma / delta
            s, p = raised, residual
        else:
            beta = gamma / gamma_prev
            alpha = gamma / (delta - beta * gamma / alpha_prev)
            s = plus(raised, beta, s)
            p = plus(residual, beta, p)
        solution_field = plus(solution_field, alpha, p)
        residual = plus(residual, -alpha, s)
        gamma_prev = gamma
        alpha_prev = alpha
    return solution_field, residual


def recentred(coefficients, step):
    out = list(coefficients)
    size = len(out)
    for i in range(size - 1):
        for k in range(size - 2, i - 1, -1):
            out[k] = out[k] + step * out[k + 1]
    return out


def finish(rows, shift_in, u0, u1, u2, u3, solution_field, residual, xs_out, rs_out, sems):
    nx, ny, nz = u3.shape
    line = gathered(rows)

    def lane(k):
        one = jnp.where(iota((8, 128), 1) == k, line, 0.0)
        return jnp.broadcast_to(jnp.sum(one, axis=1, keepdims=True), (8, 128))

    moments = [(lane(k), lane(k + 6)) for k in range(6)]
    away = to_grain(moments[1][0] / moments[0][0])
    moments = [high + low for high, low in translated(moments, -away)]
    centre = SHIFT + away
    xs, rs = steps_of(moments, centre)
    step = shift_in[...] - centre
    xs = [a[0:1, 0:1] for a in recentred(xs, step)]
    rs = [a[0:1, 0:1] for a in recentred(rs, step)]
    part = nx // PARTS
    copies = []
    for k in range(PARTS):

        def one(i, carry):
            f = (u0[i + 3, 8:-8, :], u1[i + 3, 8:-8, :], u2[i + 3, 8:-8, :], u3[i])
            xs_out[i] = xs[0] * f[0] + xs[1] * f[1] + xs[2] * f[2]
            rs_out[i] = rs[0] * f[0] + rs[1] * f[1] + rs[2] * f[2] + rs[3] * f[3]
            return carry

        lax.fori_loop(k * part, (k + 1) * part, one, 0)
        piece = pl.ds(k * part, part)
        for j, (source, target) in enumerate(((xs_out, solution_field), (rs_out, residual))):
            copy = pltpu.make_async_copy(source.at[piece], target.at[piece], sems.at[2 * k + j])
            copy.start()
            copies.append(copy)
    for copy in copies:
        copy.wait()


def shifted(a, axis, by):
    count = lax.axis_size(axis)
    pairs = [(k, k + by) for k in range(count) if 0 <= k + by < count]
    return lax.ppermute(a, axis, pairs)


def swapped(a, first):
    count = lax.axis_size(GX)
    pairs = []
    for k in range(first, count - 1, 2):
        pairs += [(k, k + 1), (k + 1, k)]
    return lax.ppermute(a, GX, pairs)


def spread(rows, axes):
    count = lax.axis_size(axes)
    out = lax.all_to_all(rows[:count].reshape(count, 1, 128), axes, 0, 0, tiled=True)
    return jnp.pad(out.reshape(count, 128), ((0, -count % 8), (0, 0)))


IN_VMEM = pl.BlockSpec(memory_space=pltpu.VMEM)
IN_HBM = pl.BlockSpec(memory_space=pltpu.HBM)


def call(body, name, outs, ins, scratch=(), aliases=None, out_specs=None, flops=0):
    return pl.pallas_call(
        body,
        out_shape=outs,
        in_specs=ins,
        out_specs=out_specs or (IN_VMEM,) * len(outs),
        scratch_shapes=list(scratch),
        input_output_aliases=aliases or {},
        compiler_params=pltpu.CompilerParams(vmem_limit_bytes=GRANT),
        cost_estimate=pl.CostEstimate(flops=flops, bytes_accessed=0, transcendentals=0) if flops else None,
        name=name,
    )


def on_device(right_side, diagonal):
    nx, ny, nz = right_side.shape
    rows = ny + 16
    shape = lambda *dims: pltpu.VMEM(dims, F32)
    field = shape(nx + 6, rows, nz)
    y_face = shape(nx + nx // 2, 8, 128)
    x_face = shape(5, ny + ny // 2, 128)
    corner = shape(3, 8, nz)
    u0, dx, yf, yb, off, on = call(
        pack,
        "pack",
        (field, field, y_face, y_face, x_face, x_face),
        (IN_HBM, IN_HBM),
        scratch=(pltpu.SemaphoreType.DMA((2,)),),
    )(*(pltpu.with_memory_space_constraint(a, pltpu.HBM) for a in (right_side, diagonal)))
    ylow = shifted(yf, "z", 1)
    yhigh = shifted(yb, "z", -1)
    off = swapped(off, 1)
    on = swapped(on, 0)
    u0, dx, coff, con = call(
        corners,
        "corners",
        (field, field, corner, corner),
        (IN_VMEM,) * 4,
        aliases={0: 0, 1: 1},
    )(u0, dx, ylow, yhigh)
    coff = swapped(coff, 1)
    con = swapped(con, 0)
    u1, u2, u3, sums, shift = call(
        middle,
        "middle",
        (field, field, shape(nx, ny, nz), shape(6, 8, nz), shape(8, 128)),
        (IN_VMEM,) * 2,
        scratch=(pltpu.VMEM((rows, nz), F32),),
        flops=20_000_000,
    )(u0, dx)
    up = lambda n: -(-n // 8) * 8
    one = lax.axis_size(FIRST)
    two = lax.axis_size(SECOND)
    u0, dx, u1, u2, u3, line = call(
        rim,
        "rim",
        (field, field, field, field, shape(nx, ny, nz), shape(up(one), 128)),
        (IN_VMEM,) * 11,
        aliases={0: 0, 1: 1, 2: 2, 3: 3, 4: 4},
    )(u0, dx, u1, u2, u3, sums, shift, off, on, coff, con)
    line = spread(line, FIRST)
    (line,) = call(regroup, "regroup", (shape(up(two), 128),), (IN_VMEM,))(line)
    line = spread(line, SECOND)
    whole = jax.ShapeDtypeStruct((nx, ny, nz), F32)
    return call(
        finish,
        "finish",
        (whole, whole),
        (IN_VMEM,) * 6,
        scratch=(pltpu.VMEM((nx, ny, nz), F32),) * 2 + (pltpu.SemaphoreType.DMA((2 * PARTS,)),),
        out_specs=(IN_HBM,) * 2,
    )(line, shift, u0, u1, u2, u3)


def solution_on(mesh, split):
    torus = Mesh(mesh.devices.reshape(*split, mesh.shape["gy"]), GX + ("z",))
    placed = (P(GX, "z", None), P(GX, "z", None))
    return jax.shard_map(on_device, mesh=torus, in_specs=placed, out_specs=placed, check_vma=False)


def solution(mesh):
    return solution_on(mesh, (8, 4, 2))
```

time: 85.7 us -> 77.3 us (0.902)
  waiting for transfers between devices: 8.18 us -> 4.94 us
  Pallas kernels: 12.3 us -> 9.38 us
  starting transfers between devices: 16.9 us -> 19.5 us
  local copies, waits for them, and re-layouts: 2.46 us -> 0 us
  blocking collectives: 44.7 us -> 42.4 us
    ppermute x0 -> x4, starting transfers between devices: none -> 16.9 us  [swapped(): return lax.ppermute(a, GX, pairs)]
    ppermute x4 -> x2, starting transfers between devices: 16.9 us -> 2.59 us  [shifted(): return lax.ppermute(a, axis, pairs)]
    ppermute x4 -> x2, waiting for transfers between devices: 8.18 us -> 4.93 us  [shifted(): return lax.ppermute(a, axis, pairs)]
    pallas_call x5 -> x6, Pallas kernels: 12.3 us -> 9.38 us  [the longest x1 3.72 us: on_device(): call(middle, 'middle', (field, field, shape(nx, ny, nz), shape(6, 8, nz),...]
    unnamed x8 -> x0, local copies, waits for them, and re-layouts: 2.46 us -> none
    all_to_all x2, blocking collectives: 44.7 us -> 42.4 us  [spread(): lax.all_to_all(rows[:count].reshape(count, 1, 128), axes, 0, 0, tiled=True)]
  transfers between devices with their start and end apart: 4 -> 6, of which waited for: 3 -> 2; matrix products, arithmetic and copies ran while one was open for 0% -> 0% of each run, Pallas kernels for 0% -> 5%
where the time goes in v3:
time: 77.3 us; the launch traced here: 77 us
  blocking collectives  42.4 us (55%)
  starting transfers between devices  19.5 us (25%)
  Pallas kernels  9.38 us (12%)
  waiting for transfers between devices  4.94 us (6%)
    all_to_all x2, blocking collectives, spread(): lax.all_to_all(rows[:count].reshape(count, 1, 128), axes, 0, 0, tiled=True)  42.4 us
    ppermute x4, starting transfers between devices, swapped(): return lax.ppermute(a, GX, pairs)  16.9 us
    ppermute x2, waiting for transfers between devices, shifted(): return lax.ppermute(a, axis, pairs)  4.93 us
    pallas_call x1, Pallas kernels, on_device(): call(middle, 'middle', (field, field, shape(nx, ny, nz), shape(6, 8, nz),...  3.72 us
    ppermute x2, starting transfers between devices, shifted(): return lax.ppermute(a, axis, pairs)  2.59 us
    pallas_call x1, Pallas kernels, on_device(): call(finish, 'finish', (whole, whole), (IN_VMEM,) * 6, scratch=(pltpu.VME...  1.89 us
    pallas_call x1, Pallas kernels, on_device(): call(rim, 'rim', (field, field, field, field, shape(nx, ny, nz), shape(up...  1.87 us
    pallas_call x1, Pallas kernels, on_device(): call(pack, 'pack', (field, field, y_face, y_face, x_face, x_face), (IN_HB...  1.72 us
  transfers between devices with their start and end apart: 6, of which 2 were waited for; matrix products, arithmetic and copies ran while one was open for 0% of the time, Pallas kernels for 5%

profile of v3, /device:TPU:1, one launch (start us, length us, event | category | flops | bytes accessed | tf_op | source)
XLA Modules:
  0.0 77.0 jit_solution(16207192581123237145)
XLA Ops:
  0.6 1.7 %pack.1 = (f32[22,80,192]{2,1,0:T(8,128)S(1)}, f32[22,80,192]{2,1,0:T(8,128)S(1)}, f32[24,8,128]{2,1,0:T(8,128)S(1)}, f32[24,8,128]{2,1,0:T(8,128)S(1)}, f32[5,9...) custom-call(f32[16,64,192]{2,1,0:T(8,128)} %b.1, f32[16,64,192]{2,1,0:T(8,128)} %d.1), custom_call_target="tpu_custom_call" | custom-call | tf_op jit(solution)/shard_map/pack/pallas_call | solution.py:444
  2.4 4.5 %collective-permute-start.2 = (f32[5,96,128]{2,1,0:T(8,128)S(1)}, f32[5,96,128]{2,1,0:T(8,128)S(1)}, u32[]{:S(2)}, u32[]{:S(2)}) collective-permute-start(f32[5,96,128]{2,1,0:T(8,128)S(1)} %get-tuple-element.33), channel_id=1, source_target_pairs={{12,24},{24,12},{36,48},{48,36},{60,72},{72,60},{84,96},{96,84},{1... | collective-permute-start | bytes 737288 | tf_op jit(solution)/shard_map/ppermute | solution.py:409
  6.9 8.6 %collective-permute-start.3 = (f32[5,96,128]{2,1,0:T(8,128)S(1)}, f32[5,96,128]{2,1,0:T(8,128)S(1)}, u32[]{:S(2)}, u32[]{:S(2)}) collective-permute-start(f32[5,96,128]{2,1,0:T(8,128)S(1)} %get-tuple-element.34), channel_id=1, source_target_pairs={{0,12},{12,0},{24,36},{36,24},{48,60},{60,48},{72,84},{84,72},{96,... | collective-permute-start | bytes 737288 | tf_op jit(solution)/shard_map/ppermute | solution.py:409
  15.4 1.3 %collective-permute-start = (f32[24,8,128]{2,1,0:T(8,128)S(1)}, f32[24,8,128]{2,1,0:T(8,128)S(1)}, u32[]{:S(2)}, u32[]{:S(2)}) collective-permute-start(f32[24,8,128]{2,1,0:T(8,128)S(1)} %get-tuple-element.24), channel_id=1, source_target_pairs={{0,1},{1,2},{2,3},{3,4},{4,5},{5,6},{6,7},{7,8},{8,9},{9,10},{10,1... | collective-permute-start | bytes 294920 | tf_op jit(solution)/shard_map/ppermute | solution.py:401
  16.7 1.3 %collective-permute-start.1 = (f32[24,8,128]{2,1,0:T(8,128)S(1)}, f32[24,8,128]{2,1,0:T(8,128)S(1)}, u32[]{:S(2)}, u32[]{:S(2)}) collective-permute-start(f32[24,8,128]{2,1,0:T(8,128)S(1)} %get-tuple-element.25), channel_id=1, source_target_pairs={{1,0},{2,1},{3,2},{4,3},{5,4},{6,5},{7,6},{8,7},{9,8},{10,9},{11,1... | collective-permute-start | bytes 294920 | tf_op jit(solution)/shard_map/ppermute | solution.py:401
  18.0 1.1 %collective-permute-done.ylow = f32[24,8,128]{2,1,0:T(8,128)S(1)} collective-permute-done((f32[24,8,128]{2,1,0:T(8,128)S(1)}, f32[24,8,128]{2,1,0:T(8,128)S(1)}, u32[]{:S(2)}, u32[]{:S(2)}) %collective-permute-start) | collective-permute-done | bytes 98336 | tf_op jit(solution)/shard_map/ppermute | solution.py:401
  19.1 3.8 %collective-permute-done.1.yhigh = f32[24,8,128]{2,1,0:T(8,128)S(1)} collective-permute-done((f32[24,8,128]{2,1,0:T(8,128)S(1)}, f32[24,8,128]{2,1,0:T(8,128)S(1)}, u32[]{:S(2)}, u32[]{:S(2)}) %collective-permute-start.1) | collective-permute-done | bytes 98336 | tf_op jit(solution)/shard_map/ppermute | solution.py:401
  23.0 0.1 corners.1
  23.1 1.9 %collective-permute-start.4 = (f32[3,8,192]{2,1,0:T(8,128)S(1)}, f32[3,8,192]{2,1,0:T(8,128)S(1)}, u32[]{:S(2)}, u32[]{:S(2)}) collective-permute-start(f32[3,8,192]{2,1,0:T(8,128)S(1)} %get-tuple-element.35), channel_id=1, source_target_pairs={{12,24},{24,12},{36,48},{48,36},{60,72},{72,60},{84,96},{96,84},{1... | collective-permute-start | bytes 55304 | tf_op jit(solution)/shard_map/ppermute | solution.py:409
  25.0 1.9 %collective-permute-start.5 = (f32[3,8,192]{2,1,0:T(8,128)S(1)}, f32[3,8,192]{2,1,0:T(8,128)S(1)}, u32[]{:S(2)}, u32[]{:S(2)}) collective-permute-start(f32[3,8,192]{2,1,0:T(8,128)S(1)} %get-tuple-element.36), channel_id=1, source_target_pairs={{0,12},{12,0},{24,36},{36,24},{48,60},{60,48},{72,84},{84,72},{96,... | collective-permute-start | bytes 55304 | tf_op jit(solution)/shard_map/ppermute | solution.py:409
  26.9 3.7 %middle.1 = (f32[22,80,192]{2,1,0:T(8,128)S(1)}, f32[22,80,192]{2,1,0:T(8,128)S(1)}, f32[16,64,192]{2,1,0:T(8,128)S(1)}, f32[6,8,192]{2,1,0:T(8,128)S(1)}, f32[8,128]{1,0:T(8,128)S(1)}) custom-call(f32[22,80,192]{2,1,0:T(8,128)S(1)} %get-tuple-element.26.u0.u0_in, f32[22,80,192]{2,1,0:T(8,128)S(1)} %get-tuple-element.27.dx.dx_in), custom_call_target="tpu_custom_call" | custom-call | flops 20000000 | tf_op jit(solution)/shard_map/middle/pallas_call | solution.py:464
  30.7 0.0 collective-permute-done.4.coff
  30.7 0.0 collective-permute-done.5.con
  30.7 0.0 collective-permute-done.2.off
  30.7 0.0 collective-permute-done.3.on
  30.7 1.9 %rim.1 = (f32[22,80,192]{2,1,0:T(8,128)S(1)}, f32[22,80,192]{2,1,0:T(8,128)S(1)}, f32[22,80,192]{2,1,0:T(8,128)S(1)}, f32[22,80,192]{2,1,0:T(8,128)S(1)}, f32[16...) custom-call(f32[22,80,192]{2,1,0:T(8,128)S(1)} %get-tuple-element.26, ...), custom_call_target="tpu_custom_call", output_to_operand_aliasing={{0}: (0, {}), {1}: (1, {}), {2}: (2, {}), {3}: (3, {}), {4}... | custom-call | tf_op jit(solution)/shard_map/rim/pallas_call | solution.py:475
  32.6 14.2 %all_to_all.10 = f32[16,1,128]{2,1,0:T(1,128)S(1)} all-to-all(f32[16,1,128]{2,1,0:T(1,128)S(1)} %bitcast.11), channel_id=1, replica_groups=mesh['y'=8,'x'=4,'c'=2,'z'=12] {'y','c'}, dimensions={0} | all-to-all | bytes 16384 | tf_op jit(solution)/shard_map/all_to_all | solution.py:414
  46.8 0.1 regroup.1
  46.9 28.2 %all_to_all.11 = f32[48,1,128]{2,1,0:T(1,128)S(1)} all-to-all(f32[48,1,128]{2,1,0:T(1,128)S(1)} %bitcast.9), channel_id=1, replica_groups=mesh['y'=8,'x'=4,'c'=2,'z'=12] {'x','z'}, dimensions={0} | all-to-all | bytes 49152 | tf_op jit(solution)/shard_map/all_to_all | solution.py:414
  75.1 1.9 %finish.1 = (f32[16,64,192]{2,1,0:T(8,128)}, f32[16,64,192]{2,1,0:T(8,128)}) custom-call(f32[48,128]{1,0:T(8,128)S(1)} %bitcast.8, f32[8,128]{1,0:T(8,128)S(1)} %get-tuple-element.32.shift_in, f32[22,80,192]{2,1,0:T(8,128)S(1)} %get-tuple-element.38.u0, f32[22,80,192]{2,1,0:T(8,128)S(1)} %get-tuple-element.39.u1, f32[22,80,192]{2,1,0:T(8,128)S(1)} %get-tuple-element.40.u2, ...), custom_call_target="tpu_custom_call" | custom-call | tf_op jit(solution)/shard_map/finish/pallas_call | solution.py:486
Async XLA Ops:
  2.4 28.3 %collective-permute-start.2 = (f32[5,96,128]{2,1,0:T(8,128)S(1)}, f32[5,96,128]{2,1,0:T(8,128)S(1)}, u32[]{:S(2)}, u32[]{:S(2)}) collective-permute-start(f32[5,96,128]{2,1,0:T(8,128)S(1)} %get-tuple-element.33), channel_id=1, source_target_pairs={{12,24},{24,12},{36,48},{48,36},{60,72},{72,60},{84,96},{96,84},{1... | collective-permute-start | bytes 737288 | tf_op jit(solution)/shard_map/ppermute | solution.py:409
  6.9 23.8 %collective-permute-start.3 = (f32[5,96,128]{2,1,0:T(8,128)S(1)}, f32[5,96,128]{2,1,0:T(8,128)S(1)}, u32[]{:S(2)}, u32[]{:S(2)}) collective-permute-start(f32[5,96,128]{2,1,0:T(8,128)S(1)} %get-tuple-element.34), channel_id=1, source_target_pairs={{0,12},{12,0},{24,36},{36,24},{48,60},{60,48},{72,84},{84,72},{96,... | collective-permute-start | bytes 737288 | tf_op jit(solution)/shard_map/ppermute | solution.py:409
  15.4 3.7 %collective-permute-start = (f32[24,8,128]{2,1,0:T(8,128)S(1)}, f32[24,8,128]{2,1,0:T(8,128)S(1)}, u32[]{:S(2)}, u32[]{:S(2)}) collective-permute-start(f32[24,8,128]{2,1,0:T(8,128)S(1)} %get-tuple-element.24), channel_id=1, source_target_pairs={{0,1},{1,2},{2,3},{3,4},{4,5},{5,6},{6,7},{7,8},{8,9},{9,10},{10,1... | collective-permute-start | bytes 294920 | tf_op jit(solution)/shard_map/ppermute | solution.py:401
  16.7 6.2 %collective-permute-start.1 = (f32[24,8,128]{2,1,0:T(8,128)S(1)}, f32[24,8,128]{2,1,0:T(8,128)S(1)}, u32[]{:S(2)}, u32[]{:S(2)}) collective-permute-start(f32[24,8,128]{2,1,0:T(8,128)S(1)} %get-tuple-element.25), channel_id=1, source_target_pairs={{1,0},{2,1},{3,2},{4,3},{5,4},{6,5},{7,6},{8,7},{9,8},{10,9},{11,1... | collective-permute-start | bytes 294920 | tf_op jit(solution)/shard_map/ppermute | solution.py:401
  23.1 7.6 %collective-permute-start.4 = (f32[3,8,192]{2,1,0:T(8,128)S(1)}, f32[3,8,192]{2,1,0:T(8,128)S(1)}, u32[]{:S(2)}, u32[]{:S(2)}) collective-permute-start(f32[3,8,192]{2,1,0:T(8,128)S(1)} %get-tuple-element.35), channel_id=1, source_target_pairs={{12,24},{24,12},{36,48},{48,36},{60,72},{72,60},{84,96},{96,84},{1... | collective-permute-start | bytes 55304 | tf_op jit(solution)/shard_map/ppermute | solution.py:409
  25.0 5.7 %collective-permute-start.5 = (f32[3,8,192]{2,1,0:T(8,128)S(1)}, f32[3,8,192]{2,1,0:T(8,128)S(1)}, u32[]{:S(2)}, u32[]{:S(2)}) collective-permute-start(f32[3,8,192]{2,1,0:T(8,128)S(1)} %get-tuple-element.36), channel_id=1, source_target_pairs={{0,12},{12,0},{24,36},{36,24},{48,60},{60,48},{72,84},{84,72},{96,... | collective-permute-start | bytes 55304 | tf_op jit(solution)/shard_map/ppermute | solution.py:409

commit v4 on v3

--- a/solution.py
+++ b/solution.py
@@ -10,8 +10,8 @@
 SHIFT = 7.0
 GRAIN = 8.0
 GX = ("y", "x", "c")
-FIRST = ("y", "c")
-SECOND = ("x", "z")
+FIRST = ("c", "z")
+SECOND = ("y", "x")
 F32 = jnp.float32
 GRANT = 24 << 20
 PARTS = 4
@@ -84,7 +84,43 @@
     return block[..., :128], rest
 
 
-def pack(b, d, u0, dx, yf, yb, off, on, sems):
+def merged(tiles, turns, first_row):
+    sub = iota(tiles[0].shape, 1)
+    width = 8 // len(turns) if len(turns) > 2 else 3
+    out = tiles[0]
+    for k in range(1, len(turns)):
+        here = pltpu.roll(tiles[k], turns[k], 1)
+        start = (k * width) if first_row else (8 - width + turns[k]) % 8
+        out = jnp.where((sub >= start) & (sub < start + width), here, out)
+    return out
+
+
+FIELD_TURNS = ((0, 5), (0, 3))
+SHIFT_TURNS = (0, 2, 4, 6)
+
+
+def pack_y(b, d, yf, yb, faces, sems):
+    nx, ny, _ = b.shape
+    copies = [
+        pltpu.make_async_copy(source.at[:, row : row + 8, :], faces.at[k], sems.at[k])
+        for k, (source, row) in enumerate(((b, ny - 8), (d, ny - 8), (b, 0), (d, 0)))
+    ]
+    for copy in copies:
+        copy.start()
+    for copy in copies:
+        copy.wait()
+    for side, out in enumerate((yf, yb)):
+        field = faces[2 * side]
+        shift = faces[2 * side + 1]
+        field = merged([field[k * nx // 2 : (k + 1) * nx // 2] for k in range(2)], FIELD_TURNS[side], side == 1)
+        shift = merged([shift[k * nx // 4 : (k + 1) * nx // 4] for k in range(4)], SHIFT_TURNS, side == 1)
+        main, rest = lanes(jnp.concatenate([field, shift], axis=0))
+        count = main.shape[0]
+        out[0:count] = main
+        out[count : count + count // 2] = squeeze(rest[: count // 2], rest[count // 2 :])
+
+
+def load(b, d, yf, u0, dx, off, on, sems):
     where = place()
     nx, ny, _ = b.shape
     copies = [
@@ -95,21 +131,8 @@
         copy.start()
     for copy in copies:
         copy.wait()
-    half = nx // 2
-
-    def y_face(row, first_row):
-        field = u0[3 : 3 + nx, row : row + 8, :]
-        shift = pltpu.roll(dx[3 : 3 + nx, row : row + 8, :], 4, 1)
-        sub = iota(field.shape, 1)
-        face = jnp.where(sub < 3 if first_row else sub >= 5, field, shift)
-        main, rest = lanes(face)
-        return main, squeeze(rest[:half], rest[half:])
-
-    for out, row, first_row in ((yf, ny, False), (yb, 8, True)):
-        main, rest = y_face(row, first_row)
-        out[0:nx] = main
-        out[nx : nx + half] = rest
     mid = ny // 2
+    own = ny // 8
     for out, high in ((off, where[0]), (on, 1 - where[0])):
         for j in range(5):
             if j < 3:
@@ -117,8 +140,9 @@
             else:
                 slab = dx[j + high * (nx - 2), 8 : 8 + ny, :]
             main, rest = lanes(slab)
-            out[j, 0:ny, :] = main
-            out[j, ny : ny + mid, :] = squeeze(rest[:mid], rest[mid:])
+            at = j * (own + own // 2)
+            out[at : at + own] = main.reshape(own, 8, 128)
+            out[at + own : at + own + own // 2] = squeeze(rest[:mid], rest[mid:]).reshape(own // 2, 8, 128)
 
 
 def unsqueeze(main, rest, second):
@@ -126,24 +150,37 @@
     return jnp.concatenate([main, rest[..., :64]], axis=-1)
 
 
-def corners(u0_in, dx_in, ylow, yhigh, u0, dx, off, on):
+def corners(u0_in, dx_in, off_in, on_in, ylow, yhigh, u0, dx, off, on):
     where = place()
     nx = u0.shape[0] - 6
     ny = u0.shape[1] - 16
-    half = nx // 2
-    for halo, row in ((ylow, 0), (yhigh, 8 + ny)):
-        for k in (0, 1):
-            part = slice(k * half, (k + 1) * half)
-            tile = unsqueeze(halo[part], halo[nx : nx + half], k == 1)
-            at = slice(3 + k * half, 3 + (k + 1) * half)
-            u0[at, row : row + 8, :] = tile
-            dx[at, row : row + 8, :] = pltpu.roll(tile, 4, 1)
+    count = nx // 2 + nx // 4
+    for side, (halo, row) in enumerate(((ylow, 0), (yhigh, 8 + ny))):
+        rest = halo[count : count + count // 2]
+        tiles = jnp.concatenate(
+            [unsqueeze(halo[: count // 2], rest, False), unsqueeze(halo[count // 2 : count], rest, True)], axis=0
+        )
+        field = tiles[: nx // 2]
+        shift = tiles[nx // 2 :]
+        for k, turn in enumerate(FIELD_TURNS[side]):
+            at = slice(3 + k * nx // 2, 3 + (k + 1) * nx // 2)
+            u0[at, row : row + 8, :] = pltpu.roll(field, 8 - turn, 1) if turn else field
+        for k, turn in enumerate(SHIFT_TURNS):
+            at = slice(3 + k * nx // 4, 3 + (k + 1) * nx // 4)
+            dx[at, row : row + 8, :] = pltpu.roll(shift, 8 - turn, 1) if turn else shift
+    start = 5 * (ny // 8 + ny // 16)
     for out, high in ((off, where[0]), (on, 1 - where[0])):
         one = 3 + high * (nx - 1)
         two = 4 + high * (nx - 3)
+        rests = []
         for j, (field, at) in enumerate(((u0, one), (u0, two), (dx, one))):
             low = field[at, 0:8, :]
-            out[j] = jnp.where(iota(low.shape, 0) >= 4, low, field[at, 8 + ny : 16 + ny, :])
+            tile = jnp.where(iota(low.shape, 0) >= 4, low, field[at, 8 + ny : 16 + ny, :])
+            main, rest = lanes(tile)
+            out[start + j] = main
+            rests.append(rest)
+        out[start + 3] = squeeze(rests[0], rests[1])
+        out[start + 4] = rests[2]
 
 
 def stencil(field, dx, at, base):
@@ -222,16 +259,19 @@
         sums_out[k] = sums[k]
 
 
-def rim(u0_in, dx_in, u1_in, u2_in, u3_in, sums_in, shift_in, off, on, coff, con, u0, dx, u1, u2, u3, row_out):
+def rim(u0_in, dx_in, u1_in, u2_in, u3_in, sums_in, shift_in, off, on, u0, dx, u1, u2, u3, row_out):
     where = place()
     nx = u0.shape[0] - 6
     ny = u0.shape[1] - 16
     mid = ny // 2
     shape = u0.shape[1:]
-    for main, corner, high in ((off, coff, where[0]), (on, con, 1 - where[0])):
+    own = ny // 8
+    start = 5 * (own + own // 2)
+    for face, high in ((off, where[0]), (on, 1 - where[0])):
         for j in range(5):
-            slab = main[j, 0:ny, :]
-            rest = main[j, ny : ny + mid, :]
+            begin = j * (own + own // 2)
+            slab = face[begin : begin + own].reshape(ny, 128)
+            rest = face[begin + own : begin + own + own // 2].reshape(mid, 128)
             top = unsqueeze(slab[:mid], rest, False)
             bottom = unsqueeze(slab[mid:], rest, True)
             field, at = (u0, j + high * (nx + 3)) if j < 3 else (dx, j - 2 + high * (nx + 2))
@@ -240,7 +280,7 @@
         one = 2 + high * (nx + 1)
         two = 1 + high * (nx + 3)
         for j, (field, at) in enumerate(((u0, one), (u0, two), (dx, one))):
-            tile = corner[j]
+            tile = unsqueeze(face[start + j], face[start + 3 + j // 2], j == 1)
             field[at, 0:8, :] = tile
             field[at, 8 + ny : 16 + ny, :] = tile
     keep = side_mask(where, shape)
@@ -438,29 +478,35 @@
     rows = ny + 16
     shape = lambda *dims: pltpu.VMEM(dims, F32)
     field = shape(nx + 6, rows, nz)
-    y_face = shape(nx + nx // 2, 8, 128)
-    x_face = shape(5, ny + ny // 2, 128)
-    corner = shape(3, 8, nz)
-    u0, dx, yf, yb, off, on = call(
-        pack,
-        "pack",
-        (field, field, y_face, y_face, x_face, x_face),
+    y_face = shape((nx // 2 + nx // 4) * 3 // 2, 8, 128)
+    x_face = shape(5 * (ny // 8 + ny // 16) + 5, 8, 128)
+    right_side, diagonal = (pltpu.with_memory_space_constraint(a, pltpu.HBM) for a in (right_side, diagonal))
+    yf, yb = call(
+        pack_y,
+        "pack_y",
+        (y_face, y_face),
         (IN_HBM, IN_HBM),
-        scratch=(pltpu.SemaphoreType.DMA((2,)),),
-    )(*(pltpu.with_memory_space_constraint(a, pltpu.HBM) for a in (right_side, diagonal)))
+        scratch=(pltpu.VMEM((4, nx, 8, nz), F32), pltpu.SemaphoreType.DMA((4,))),
+    )(right_side, diagonal)
     ylow = shifted(yf, "z", 1)
     yhigh = shifted(yb, "z", -1)
+    u0, dx, off, on = call(
+        load,
+        "load",
+        (field, field, x_face, x_face),
+        (IN_HBM, IN_HBM, IN_VMEM),
+        scratch=(pltpu.SemaphoreType.DMA((2,)),),
+        flops=10_000_000,
+    )(right_side, diagonal, yf)
+    u0, dx, off, on = call(
+        corners,
+        "corners",
+        (field, field, x_face, x_face),
+        (IN_VMEM,) * 6,
+        aliases={k: k for k in range(4)},
+    )(u0, dx, off, on, ylow, yhigh)
     off = swapped(off, 1)
     on = swapped(on, 0)
-    u0, dx, coff, con = call(
-        corners,
-        "corners",
-        (field, field, corner, corner),
-        (IN_VMEM,) * 4,
-        aliases={0: 0, 1: 1},
-    )(u0, dx, ylow, yhigh)
-    coff = swapped(coff, 1)
-    con = swapped(con, 0)
     u1, u2, u3, sums, shift = call(
         middle,
         "middle",
@@ -476,9 +522,9 @@
         rim,
         "rim",
         (field, field, field, field, shape(nx, ny, nz), shape(up(one), 128)),
-        (IN_VMEM,) * 11,
-        aliases={0: 0, 1: 1, 2: 2, 3: 3, 4: 4},
-    )(u0, dx, u1, u2, u3, sums, shift, off, on, coff, con)
+        (IN_VMEM,) * 9,
+        aliases={k: k for k in range(5)},
+    )(u0, dx, u1, u2, u3, sums, shift, off, on)
     line = spread(line, FIRST)
     (line,) = call(regroup, "regroup", (shape(up(two), 128),), (IN_VMEM,))(line)
     line = spread(line, SECOND)

time: 77.3 us -> 68.9 us (0.89)
  waiting for transfers between devices: 4.94 us -> 0.01 us
  blocking collectives: 42.4 us -> 38.1 us
  Pallas kernels: 9.38 us -> 10.6 us
    ppermute x2, waiting for transfers between devices: 4.93 us -> 0.01 us  [shifted(): return lax.ppermute(a, axis, pairs)]
    ppermute x4 -> x2, starting transfers between devices: 16.9 us -> 12.4 us  [swapped(): return lax.ppermute(a, GX, pairs)]
    all_to_all x2, blocking collectives: 42.4 us -> 38.1 us  [spread(): lax.all_to_all(rows[:count].reshape(count, 1, 128), axes, 0, 0, tiled=True)]
    ppermute x2, starting transfers between devices: 2.59 us -> 6.74 us  [shifted(): return lax.ppermute(a, axis, pairs)]
    pallas_call x2 -> x3, Pallas kernels: 1.81 us -> 3.06 us  [the longest x1 1.68 us: on_device(): call(load, 'load', (field, field, x_face, x_face), (IN_HBM, IN_HBM, IN_VM...]
  transfers between devices with their start and end apart: 6 -> 4, of which waited for: 2 -> 0; matrix products, arithmetic and copies ran while one was open for 0% -> 0% of each run, Pallas kernels for 5% -> 8%
where the time goes in v4:
time: 68.9 us; the launch traced here: 68.6 us
  blocking collectives  38.1 us (55%)
  starting transfers between devices  19.1 us (28%)
  Pallas kernels  10.6 us (15%)
  between operations  0.72 us (1%)
    all_to_all x2, blocking collectives, spread(): lax.all_to_all(rows[:count].reshape(count, 1, 128), axes, 0, 0, tiled=True)  38.1 us
    ppermute x2, starting transfers between devices, swapped(): return lax.ppermute(a, GX, pairs)  12.4 us
    ppermute x2, starting transfers between devices, shifted(): return lax.ppermute(a, axis, pairs)  6.74 us
    pallas_call x1, Pallas kernels, on_device(): call(middle, 'middle', (field, field, shape(nx, ny, nz), shape(6, 8, nz),...  3.71 us
    pallas_call x1, Pallas kernels, on_device(): call(finish, 'finish', (whole, whole), (IN_VMEM,) * 6, scratch=(pltpu.VME...  1.89 us
    pallas_call x1, Pallas kernels, on_device(): call(rim, 'rim', (field, field, field, field, shape(nx, ny, nz), shape(up...  1.85 us
    pallas_call x1, Pallas kernels, on_device(): call(load, 'load', (field, field, x_face, x_face), (IN_HBM, IN_HBM, IN_VM...  1.68 us
  transfers between devices with their start and end apart: 4, of which 0 were waited for; matrix products, arithmetic and copies ran while one was open for 0% of the time, Pallas kernels for 8%

profile of v4, /device:TPU:1, one launch (start us, length us, event | category | flops | bytes accessed | tf_op | source)
XLA Modules:
  0.0 68.6 jit_solution(5150728795454790898)
XLA Ops:
  0.6 1.2 %pack_y.1 = (f32[18,8,128]{2,1,0:T(8,128)S(1)}, f32[18,8,128]{2,1,0:T(8,128)S(1)}) custom-call(f32[16,64,192]{2,1,0:T(8,128)} %b.3, f32[16,64,192]{2,1,0:T(8,128)} %d.3), custom_call_target="tpu_custom_call" | custom-call | tf_op jit(solution)/shard_map/pack_y/pallas_call | solution.py:484
  1.9 1.3 %collective-permute-start.1 = (f32[18,8,128]{2,1,0:T(8,128)S(1)}, f32[18,8,128]{2,1,0:T(8,128)S(1)}, u32[]{:S(2)}, u32[]{:S(2)}) collective-permute-start(f32[18,8,128]{2,1,0:T(8,128)S(1)} %get-tuple-element.27), channel_id=1, source_target_pairs={{1,0},{2,1},{3,2},{4,3},{5,4},{6,5},{7,6},{8,7},{9,8},{10,9},{11,1... | collective-permute-start | bytes 221192 | tf_op jit(solution)/shard_map/ppermute | solution.py:441
  3.2 5.4 %collective-permute-start = (f32[18,8,128]{2,1,0:T(8,128)S(1)}, f32[18,8,128]{2,1,0:T(8,128)S(1)}, u32[]{:S(2)}, u32[]{:S(2)}) collective-permute-start(f32[18,8,128]{2,1,0:T(8,128)S(1)} %get-tuple-element.22.yf), channel_id=1, source_target_pairs={{0,1},{1,2},{2,3},{3,4},{4,5},{5,6},{6,7},{7,8},{8,9},{9,10},{10,1... | collective-permute-start | bytes 221192 | tf_op jit(solution)/shard_map/ppermute | solution.py:441
  8.6 1.7 %load.1 = (f32[22,80,192]{2,1,0:T(8,128)S(1)}, f32[22,80,192]{2,1,0:T(8,128)S(1)}, f32[65,8,128]{2,1,0:T(8,128)S(1)}, f32[65,8,128]{2,1,0:T(8,128)S(1)}) custom-call(f32[16,64,192]{2,1,0:T(8,128)} %b.3, f32[16,64,192]{2,1,0:T(8,128)} %d.3, f32[18,8,128]{2,1,0:T(8,128)S(1)} %get-tuple-element.22.yf), custom_call_target="tpu_custom_call" | custom-call | flops 10000000 | tf_op jit(solution)/shard_map/load/pallas_call | solution.py:493
  10.3 0.0 collective-permute-done.1.yhigh
  10.3 0.0 collective-permute-done.ylow
  10.3 0.2 corners.1
  10.5 4.2 %collective-permute-start.2 = (f32[65,8,128]{2,1,0:T(8,128)S(1)}, f32[65,8,128]{2,1,0:T(8,128)S(1)}, u32[]{:S(2)}, u32[]{:S(2)}) collective-permute-start(f32[65,8,128]{2,1,0:T(8,128)S(1)} %get-tuple-element.35), channel_id=1, source_target_pairs={{12,24},{24,12},{36,48},{48,36},{60,72},{72,60},{84,96},{96,84},{1... | collective-permute-start | bytes 798728 | tf_op jit(solution)/shard_map/ppermute | solution.py:449
  14.7 8.2 %collective-permute-start.3 = (f32[65,8,128]{2,1,0:T(8,128)S(1)}, f32[65,8,128]{2,1,0:T(8,128)S(1)}, u32[]{:S(2)}, u32[]{:S(2)}) collective-permute-start(f32[65,8,128]{2,1,0:T(8,128)S(1)} %get-tuple-element.36), channel_id=1, source_target_pairs={{0,12},{12,0},{24,36},{36,24},{48,60},{60,48},{72,84},{84,72},{96,... | collective-permute-start | bytes 798728 | tf_op jit(solution)/shard_map/ppermute | solution.py:449
  22.9 3.7 %middle.1 = (f32[22,80,192]{2,1,0:T(8,128)S(1)}, f32[22,80,192]{2,1,0:T(8,128)S(1)}, f32[16,64,192]{2,1,0:T(8,128)S(1)}, f32[6,8,192]{2,1,0:T(8,128)S(1)}, f32[8,128]{1,0:T(8,128)S(1)}) custom-call(f32[22,80,192]{2,1,0:T(8,128)S(1)} %get-tuple-element.28.u0.u0_in, f32[22,80,192]{2,1,0:T(8,128)S(1)} %get-tuple-element.29.dx.dx_in), custom_call_target="tpu_custom_call" | custom-call | flops 20000000 | tf_op jit(solution)/shard_map/middle/pallas_call | solution.py:510
  26.6 0.0 collective-permute-done.2.off
  26.6 0.0 collective-permute-done.3.on
  26.6 1.9 %rim.1 = (f32[22,80,192]{2,1,0:T(8,128)S(1)}, f32[22,80,192]{2,1,0:T(8,128)S(1)}, f32[22,80,192]{2,1,0:T(8,128)S(1)}, f32[22,80,192]{2,1,0:T(8,128)S(1)}, f32[16...) custom-call(f32[22,80,192]{2,1,0:T(8,128)S(1)} %get-tuple-element.28, ...), custom_call_target="tpu_custom_call", output_to_operand_aliasing={{0}: (0, {}), {1}: (1, {}), {2}: (2, {}), {3}: (3, {}), {4}... | custom-call | tf_op jit(solution)/shard_map/rim/pallas_call | solution.py:521
  28.5 20.3 %all_to_all.10 = f32[24,1,128]{2,1,0:T(1,128)S(1)} all-to-all(f32[24,1,128]{2,1,0:T(1,128)S(1)} %bitcast.11), channel_id=1, replica_groups=mesh['y'=8,'x'=4,'c'=2,'z'=12] {'c','z'}, dimensions={0} | all-to-all | bytes 24576 | tf_op jit(solution)/shard_map/all_to_all | solution.py:454
  48.8 0.1 regroup.1
  48.9 17.8 %all_to_all.11 = f32[32,1,128]{2,1,0:T(1,128)S(1)} all-to-all(f32[32,1,128]{2,1,0:T(1,128)S(1)} %bitcast.9), channel_id=1, replica_groups=mesh['y'=8,'x'=4,'c'=2,'z'=12] {'y','x'}, dimensions={0} | all-to-all | bytes 32768 | tf_op jit(solution)/shard_map/all_to_all | solution.py:454
  66.7 1.9 %finish.1 = (f32[16,64,192]{2,1,0:T(8,128)}, f32[16,64,192]{2,1,0:T(8,128)}) custom-call(f32[32,128]{1,0:T(8,128)S(1)} %bitcast.8, f32[8,128]{1,0:T(8,128)S(1)} %get-tuple-element.34.shift_in, f32[22,80,192]{2,1,0:T(8,128)S(1)} %get-tuple-element.38.u0, f32[22,80,192]{2,1,0:T(8,128)S(1)} %get-tuple-element.39.u1, f32[22,80,192]{2,1,0:T(8,128)S(1)} %get-tuple-element.40.u2, ...), custom_call_target="tpu_custom_call" | custom-call | tf_op jit(solution)/shard_map/finish/pallas_call | solution.py:532
Async XLA Ops:
  1.9 8.4 %collective-permute-start.1 = (f32[18,8,128]{2,1,0:T(8,128)S(1)}, f32[18,8,128]{2,1,0:T(8,128)S(1)}, u32[]{:S(2)}, u32[]{:S(2)}) collective-permute-start(f32[18,8,128]{2,1,0:T(8,128)S(1)} %get-tuple-element.27), channel_id=1, source_target_pairs={{1,0},{2,1},{3,2},{4,3},{5,4},{6,5},{7,6},{8,7},{9,8},{10,9},{11,1... | collective-permute-start | bytes 221192 | tf_op jit(solution)/shard_map/ppermute | solution.py:441
  3.2 7.2 %collective-permute-start = (f32[18,8,128]{2,1,0:T(8,128)S(1)}, f32[18,8,128]{2,1,0:T(8,128)S(1)}, u32[]{:S(2)}, u32[]{:S(2)}) collective-permute-start(f32[18,8,128]{2,1,0:T(8,128)S(1)} %get-tuple-element.22.yf), channel_id=1, source_target_pairs={{0,1},{1,2},{2,3},{3,4},{4,5},{5,6},{6,7},{7,8},{8,9},{9,10},{10,1... | collective-permute-start | bytes 221192 | tf_op jit(solution)/shard_map/ppermute | solution.py:441
  10.5 16.1 %collective-permute-start.2 = (f32[65,8,128]{2,1,0:T(8,128)S(1)}, f32[65,8,128]{2,1,0:T(8,128)S(1)}, u32[]{:S(2)}, u32[]{:S(2)}) collective-permute-start(f32[65,8,128]{2,1,0:T(8,128)S(1)} %get-tuple-element.35), channel_id=1, source_target_pairs={{12,24},{24,12},{36,48},{48,36},{60,72},{72,60},{84,96},{96,84},{1... | collective-permute-start | bytes 798728 | tf_op jit(solution)/shard_map/ppermute | solution.py:449
  14.7 11.9 %collective-permute-start.3 = (f32[65,8,128]{2,1,0:T(8,128)S(1)}, f32[65,8,128]{2,1,0:T(8,128)S(1)}, u32[]{:S(2)}, u32[]{:S(2)}) collective-permute-start(f32[65,8,128]{2,1,0:T(8,128)S(1)} %get-tuple-element.36), channel_id=1, source_target_pairs={{0,12},{12,0},{24,36},{36,24},{48,60},{60,48},{72,84},{84,72},{96,... | collective-permute-start | bytes 798728 | tf_op jit(solution)/shard_map/ppermute | solution.py:449

commit v5 on v4

--- a/solution.py
+++ b/solution.py
@@ -15,6 +15,8 @@
 F32 = jnp.float32
 GRANT = 24 << 20
 PARTS = 4
+PART = 16
+TOP = 16
 
 
 def two_sum(a, b):
@@ -99,7 +101,8 @@
 SHIFT_TURNS = (0, 2, 4, 6)
 
 
-def pack_y(b, d, yf, yb, faces, sems):
+def pack_y(b, d, one, two, faces, sems):
+    even = lax.axis_index("z") % 2 == 0
     nx, ny, _ = b.shape
     copies = [
         pltpu.make_async_copy(source.at[:, row : row + 8, :], faces.at[k], sems.at[k])
@@ -109,127 +112,157 @@
         copy.start()
     for copy in copies:
         copy.wait()
-    for side, out in enumerate((yf, yb)):
+    done = []
+    for side in range(2):
         field = faces[2 * side]
         shift = faces[2 * side + 1]
         field = merged([field[k * nx // 2 : (k + 1) * nx // 2] for k in range(2)], FIELD_TURNS[side], side == 1)
         shift = merged([shift[k * nx // 4 : (k + 1) * nx // 4] for k in range(4)], SHIFT_TURNS, side == 1)
         main, rest = lanes(jnp.concatenate([field, shift], axis=0))
         count = main.shape[0]
-        out[0:count] = main
-        out[count : count + count // 2] = squeeze(rest[: count // 2], rest[count // 2 :])
-
-
-def load(b, d, yf, u0, dx, off, on, sems):
+        done.append(jnp.concatenate([main, squeeze(rest[: count // 2], rest[count // 2 :])], axis=0))
+    one[...] = jnp.where(even, done[0], done[1])
+    two[...] = jnp.where(even, done[1], done[0])
+
+
+def load(b, d, face, u0, dx, off, on, stage, sems):
     where = place()
     nx, ny, _ = b.shape
-    copies = [
-        pltpu.make_async_copy(source, target.at[3 : 3 + nx, 8 : 8 + ny, :], sems.at[k])
-        for k, (source, target) in enumerate(((b, u0), (d, dx)))
-    ]
+    copies = [pltpu.make_async_copy(source, stage.at[k], sems.at[k]) for k, source in enumerate((b, d))]
     for copy in copies:
         copy.start()
-    for copy in copies:
+    for k, (copy, into) in enumerate(zip(copies, (u0, dx))):
         copy.wait()
+
+        def one(i, carry):
+            main, rest = lanes(stage[k, i])
+            into[0, i + 3, TOP : TOP + ny, :] = main
+            into[1, i + 3, TOP : TOP + ny, :] = rest
+            return carry
+
+        lax.fori_loop(0, nx, one, 0, unroll=2)
     mid = ny // 2
     own = ny // 8
     for out, high in ((off, where[0]), (on, 1 - where[0])):
         for j in range(5):
-            if j < 3:
-                slab = u0[3 + j + high * (nx - 3), 8 : 8 + ny, :]
-            else:
-                slab = dx[j + high * (nx - 2), 8 : 8 + ny, :]
-            main, rest = lanes(slab)
+            into, slab = (u0, 3 + j + high * (nx - 3)) if j < 3 else (dx, j + high * (nx - 2))
             at = j * (own + own // 2)
-            out[at : at + own] = main.reshape(own, 8, 128)
-            out[at + own : at + own + own // 2] = squeeze(rest[:mid], rest[mid:]).reshape(own // 2, 8, 128)
-
-
-def unsqueeze(main, rest, second):
+            out[at : at + own] = into[0, slab, TOP : TOP + ny, :].reshape(own, 8, 128)
+            rest = into[1, slab, TOP : TOP + ny, :]
+            out[at + own : at + own + own // 2] = (rest[:mid] + half_turn(rest[mid:])).reshape(own // 2, 8, 128)
+
+
+def lone(rest, second):
     rest = half_turn(rest) if second else rest
-    return jnp.concatenate([main, rest[..., :64]], axis=-1)
-
-
-def corners(u0_in, dx_in, off_in, on_in, ylow, yhigh, u0, dx, off, on):
+    return jnp.where(lax.broadcasted_iota(jnp.int32, rest.shape, rest.ndim - 1) < 64, rest, 0.0)
+
+
+def corners(u0_in, dx_in, off_in, on_in, got_one, got_two, u0, dx, off, on):
     where = place()
-    nx = u0.shape[0] - 6
-    ny = u0.shape[1] - 16
+    even = lax.axis_index("z") % 2 == 0
+    nx = u0.shape[1] - 6
+    ny = u0.shape[2] - 2 * TOP
     count = nx // 2 + nx // 4
-    for side, (halo, row) in enumerate(((ylow, 0), (yhigh, 8 + ny))):
-        rest = halo[count : count + count // 2]
-        tiles = jnp.concatenate(
-            [unsqueeze(halo[: count // 2], rest, False), unsqueeze(halo[count // 2 : count], rest, True)], axis=0
-        )
-        field = tiles[: nx // 2]
-        shift = tiles[nx // 2 :]
-        for k, turn in enumerate(FIELD_TURNS[side]):
-            at = slice(3 + k * nx // 2, 3 + (k + 1) * nx // 2)
-            u0[at, row : row + 8, :] = pltpu.roll(field, 8 - turn, 1) if turn else field
-        for k, turn in enumerate(SHIFT_TURNS):
-            at = slice(3 + k * nx // 4, 3 + (k + 1) * nx // 4)
-            dx[at, row : row + 8, :] = pltpu.roll(shift, 8 - turn, 1) if turn else shift
+    half = count // 2
+    for side, row in enumerate((TOP - 8, TOP + ny)):
+        first, second = (got_two, got_one) if side == 0 else (got_one, got_two)
+        halo = jnp.where(even, first[...], second[...])
+        rest = halo[count : count + half]
+        for plane, tiles in enumerate((halo[:count], jnp.concatenate([lone(rest, False), lone(rest, True)], axis=0))):
+            field = tiles[: nx // 2]
+            shift = tiles[nx // 2 :]
+            for k, turn in enumerate(FIELD_TURNS[side]):
+                at = slice(3 + k * nx // 2, 3 + (k + 1) * nx // 2)
+                u0[plane, at, row : row + 8, :] = pltpu.roll(field, 8 - turn, 1) if turn else field
+            for k, turn in enumerate(SHIFT_TURNS):
+                at = slice(3 + k * nx // 4, 3 + (k + 1) * nx // 4)
+                dx[plane, at, row : row + 8, :] = pltpu.roll(shift, 8 - turn, 1) if turn else shift
     start = 5 * (ny // 8 + ny // 16)
     for out, high in ((off, where[0]), (on, 1 - where[0])):
         one = 3 + high * (nx - 1)
         two = 4 + high * (nx - 3)
         rests = []
         for j, (field, at) in enumerate(((u0, one), (u0, two), (dx, one))):
-            low = field[at, 0:8, :]
-            tile = jnp.where(iota(low.shape, 0) >= 4, low, field[at, 8 + ny : 16 + ny, :])
-            main, rest = lanes(tile)
-            out[start + j] = main
-            rests.append(rest)
+            tiles = []
+            for plane in range(2):
+                low = field[plane, at, TOP - 8 : TOP, :]
+                tiles.append(jnp.where(iota(low.shape, 0) >= 4, low, field[plane, at, TOP + ny : TOP + ny + 8, :]))
+            out[start + j] = tiles[0]
+            rests.append(tiles[1])
         out[start + 3] = squeeze(rests[0], rests[1])
         out[start + 4] = rests[2]
 
 
-def stencil(field, dx, at, base):
-    mid = field[at]
-    rows = mid.shape[0]
-    padded = jnp.pad(mid, ((0, 0), (0, 256 - mid.shape[1])))
-    beside = field[at - 1] + field[at + 1]
-    beside = beside + (pltpu.roll(mid, 1, 0) + pltpu.roll(mid, rows - 1, 0))
-    across = pltpu.roll(padded, 1, 1) + pltpu.roll(padded, 255, 1)
-    return (dx[at] + base) * mid - (beside + across[:, : mid.shape[1]])
+def stencil(field, dx, at, base, row, rows):
+    here = slice(row, row + rows)
+    above = slice(row - 1, row + rows - 1)
+    below = slice(row + 1, row + rows + 1)
+    lane = iota((rows, 128), 1)
+    mid = [field[p, at, here, :] for p in range(2)]
+    beside = [
+        (field[p, at - 1, here, :] + field[p, at + 1, here, :]) + (field[p, at, above, :] + field[p, at, below, :])
+        for p in range(2)
+    ]
+    right = [pltpu.roll(a, 1, 1) for a in mid]
+    left = [pltpu.roll(a, 127, 1) for a in mid]
+    across = (
+        jnp.where(lane == 0, right[1], right[0]) + jnp.where(lane == 127, left[1], left[0]),
+        jnp.where(lane == 0, right[0], right[1]) + left[1],
+    )
+    new = [(dx[p, at, here, :] + base) * mid[p] - (beside[p] + across[p]) for p in range(2)]
+    return new[0], jnp.where(lane < 64, new[1], 0.0)
 
 
 def fold(a):
-    rows = a.shape[0] - 16
-    return jnp.sum(a[8 : 8 + rows].reshape(rows // 8, 8, a.shape[1]), axis=0)
+    return jnp.sum(a.reshape(-1, 8, 128), axis=0)
 
 
 def total(a):
     return jnp.broadcast_to(jnp.sum(a, axis=(0, 1), keepdims=True), (8, 128))
 
 
-def side_mask(where, shape):
-    rows = iota(shape, 0)
-    low = jnp.full(shape, where[3].astype(F32))
-    high = jnp.full(shape, where[4].astype(F32))
-    return jnp.where(rows < 8, low, jnp.where(rows >= shape[0] - 8, high, 1.0))
-
-
-def products(f0, f1, f2, f3):
-    return tuple(fold(p) for p in (f0 * f0, f0 * f1, f1 * f1, f1 * f2, f2 * f2)) + (
-        jnp.sum((f2[8:-8] * f3).reshape(-1, 8, f3.shape[1]), axis=0),
-    )
-
-
-def accumulated(sums, more):
-    return tuple(a + b for a, b in zip(sums, more))
-
-
-def middle(u0, dx, u1, u2, u3, sums_out, shift_out, keep):
+def raised(into, field, dx, at, base, there, factor=None):
+    ny = field.shape[2] - 2 * TOP
+    for row in range(TOP, TOP + ny, PART):
+        for p, new in enumerate(stencil(field, dx, at, base, row, PART)):
+            into[p, at, row : row + PART, :] = new if factor is None else new * factor
+    for row, edge in ((TOP - 8, there[0]), (TOP + ny, there[1])):
+        edge = edge if factor is None else edge * factor
+        for p, new in enumerate(stencil(field, dx, at, base, row, 8)):
+            into[p, at, row : row + 8, :] = new * edge
+
+
+def summed(u0, dx, u1, u2, u3, at, base, sums):
+    ny = u0.shape[2] - 2 * TOP
+    sums = list(sums)
+    for row in range(TOP, TOP + ny, PART):
+        here = slice(row, row + PART)
+        for p, f3 in enumerate(stencil(u2, dx, at, base, row, PART)):
+            u3[p, at - 3, row - TOP : row - TOP + PART, :] = f3
+            f0 = u0[p, at, here, :]
+            f1 = u1[p, at, here, :]
+            f2 = u2[p, at, here, :]
+            for k, product in enumerate((f0 * f0, f0 * f1, f1 * f1, f1 * f2, f2 * f2, f2 * f3)):
+                sums[k] = sums[k] + fold(product)
+    return tuple(sums)
+
+
+def middle(u0, dx, u1, u2, u3, sums_out, shift_out):
     where = place()
-    nx = u0.shape[0] - 6
-    shape = u0.shape[1:]
-    zero = jnp.zeros((8, shape[1]), F32)
-    keep[...] = side_mask(where, shape)
+    nx = u0.shape[1] - 6
+    ny = u0.shape[2] - 2 * TOP
+    there = [where[k].astype(F32) for k in (3, 4)]
+    zero = jnp.zeros((8, 128), F32)
 
     def probe(i, carry):
+        norm, lift = carry
         at = 5 + 3 * i
-        mid = u0[at]
-        return carry[0] + fold(mid * mid), carry[1] + fold(mid * stencil(u0, dx, at, 6.0))
+        for row in range(TOP, TOP + ny, PART):
+            for p, new in enumerate(stencil(u0, dx, at, 6.0, row, PART)):
+                mid = u0[p, at, row : row + PART, :]
+                norm = norm + fold(mid * mid)
+                lift = lift + fold(mid * new)
+        return norm, lift
 
     norm, lift = lax.fori_loop(0, 4, probe, (zero, zero), unroll=2)
     norm = total(norm)
@@ -237,20 +270,18 @@
     shift = jnp.where(norm > 0.0, lift / jnp.where(norm > 0.0, norm, 1.0), SHIFT)
     shift = to_grain(jnp.clip(shift, 0.0, 14.0))
     shift_out[...] = shift
-    base = 6.0 - shift[0:1, 0:1]
+    base = 6.0 - shift[0:1, :]
 
     def first(i, carry):
-        u1[i] = stencil(u0, dx, i, base) * keep[...]
+        raised(u1, u0, dx, i, base, there)
         return carry
 
     def second(i, carry):
-        u2[i] = stencil(u1, dx, i, base) * keep[...]
+        raised(u2, u1, dx, i, base, there)
         return carry
 
     def third(i, sums):
-        new = stencil(u2, dx, i, base)[8:-8]
-        u3[i - 3] = new
-        return accumulated(sums, products(u0[i], u1[i], u2[i], new))
+        return summed(u0, dx, u1, u2, u3, i, base, sums)
 
     lax.fori_loop(4, nx + 2, first, 0, unroll=2)
     lax.fori_loop(5, nx + 1, second, 0, unroll=2)
@@ -261,49 +292,44 @@
 
 def rim(u0_in, dx_in, u1_in, u2_in, u3_in, sums_in, shift_in, off, on, u0, dx, u1, u2, u3, row_out):
     where = place()
-    nx = u0.shape[0] - 6
-    ny = u0.shape[1] - 16
+    nx = u0.shape[1] - 6
+    ny = u0.shape[2] - 2 * TOP
+    there = [where[k].astype(F32) for k in (3, 4)]
     mid = ny // 2
-    shape = u0.shape[1:]
     own = ny // 8
     start = 5 * (own + own // 2)
     for face, high in ((off, where[0]), (on, 1 - where[0])):
         for j in range(5):
             begin = j * (own + own // 2)
-            slab = face[begin : begin + own].reshape(ny, 128)
             rest = face[begin + own : begin + own + own // 2].reshape(mid, 128)
-            top = unsqueeze(slab[:mid], rest, False)
-            bottom = unsqueeze(slab[mid:], rest, True)
             field, at = (u0, j + high * (nx + 3)) if j < 3 else (dx, j - 2 + high * (nx + 2))
-            field[at, 8 : 8 + mid, :] = top
-            field[at, 8 + mid : 8 + ny, :] = bottom
+            field[0, at, TOP : TOP + ny, :] = face[begin : begin + own].reshape(ny, 128)
+            field[1, at, TOP : TOP + mid, :] = lone(rest, False)
+            field[1, at, TOP + mid : TOP + ny, :] = lone(rest, True)
         one = 2 + high * (nx + 1)
         two = 1 + high * (nx + 3)
         for j, (field, at) in enumerate(((u0, one), (u0, two), (dx, one))):
-            tile = unsqueeze(face[start + j], face[start + 3 + j // 2], j == 1)
-            field[at, 0:8, :] = tile
-            field[at, 8 + ny : 16 + ny, :] = tile
-    keep = side_mask(where, shape)
+            for plane, tile in enumerate((face[start + j], lone(face[start + 3 + j // 2], j == 1))):
+                field[plane, at, TOP - 8 : TOP, :] = tile
+                field[plane, at, TOP + ny : TOP + ny + 8, :] = tile
     shift = shift_in[...]
-    base = 6.0 - shift[0:1, 0:1]
+    base = 6.0 - shift[0:1, :]
     low = where[1].astype(F32)
     high = where[2].astype(F32)
 
     def first(i, carry):
-        u1[1 + i] = stencil(u0, dx, 1 + i, base) * (keep * jnp.where(i < 2, low, 1.0))
-        u1[nx + 2 + i] = stencil(u0, dx, nx + 2 + i, base) * (keep * jnp.where(i > 0, high, 1.0))
+        raised(u1, u0, dx, 1 + i, base, there, jnp.where(i < 2, low, 1.0))
+        raised(u1, u0, dx, nx + 2 + i, base, there, jnp.where(i > 0, high, 1.0))
         return carry
 
     def second(i, carry):
-        u2[2 + i] = stencil(u1, dx, 2 + i, base) * (keep * jnp.where(i < 1, low, 1.0))
-        u2[nx + 1 + i] = stencil(u1, dx, nx + 1 + i, base) * (keep * jnp.where(i > 1, high, 1.0))
+        raised(u2, u1, dx, 2 + i, base, there, jnp.where(i < 1, low, 1.0))
+        raised(u2, u1, dx, nx + 1 + i, base, there, jnp.where(i > 1, high, 1.0))
         return carry
 
     def third(i, sums):
         for at in (3 + i, nx + i):
-            new = stencil(u2, dx, at, base)[8:-8]
-            u3[at - 3] = new
-            sums = accumulated(sums, products(u0[at], u1[at], u2[at], new))
+            sums = summed(u0, dx, u1, u2, u3, at, base, sums)
         return sums
 
     lax.fori_loop(0, 3, first, 0)
@@ -400,7 +426,7 @@
 
 
 def finish(rows, shift_in, u0, u1, u2, u3, solution_field, residual, xs_out, rs_out, sems):
-    nx, ny, nz = u3.shape
+    nx, ny, nz = xs_out.shape
     line = gathered(rows)
 
     def lane(k):
@@ -413,16 +439,20 @@
     centre = SHIFT + away
     xs, rs = steps_of(moments, centre)
     step = shift_in[...] - centre
-    xs = [a[0:1, 0:1] for a in recentred(xs, step)]
-    rs = [a[0:1, 0:1] for a in recentred(rs, step)]
+    xs = [a[0:1, :] for a in recentred(xs, step)]
+    rs = [a[0:1, :] for a in recentred(rs, step)]
     part = nx // PARTS
     copies = []
     for k in range(PARTS):
 
         def one(i, carry):
-            f = (u0[i + 3, 8:-8, :], u1[i + 3, 8:-8, :], u2[i + 3, 8:-8, :], u3[i])
-            xs_out[i] = xs[0] * f[0] + xs[1] * f[1] + xs[2] * f[2]
-            rs_out[i] = rs[0] * f[0] + rs[1] * f[1] + rs[2] * f[2] + rs[3] * f[3]
+            for p, (begin, width) in enumerate(((0, 128), (128, nz - 128))):
+                own = pl.ds(TOP, ny)
+                f = (u0[p, i + 3, own, :], u1[p, i + 3, own, :], u2[p, i + 3, own, :], u3[p, i])
+                x = (xs[0] * f[0] + xs[1] * f[1]) + xs[2] * f[2]
+                r = (rs[0] * f[0] + rs[1] * f[1]) + (rs[2] * f[2] + rs[3] * f[3])
+                xs_out[i, :, begin : begin + width] = x[:, :width]
+                rs_out[i, :, begin : begin + width] = r[:, :width]
             return carry
 
         lax.fori_loop(k * part, (k + 1) * part, one, 0)
@@ -435,18 +465,12 @@
         copy.wait()
 
 
-def shifted(a, axis, by):
+def swapped(a, axis, first):
     count = lax.axis_size(axis)
-    pairs = [(k, k + by) for k in range(count) if 0 <= k + by < count]
-    return lax.ppermute(a, axis, pairs)
-
-
-def swapped(a, first):
-    count = lax.axis_size(GX)
     pairs = []
     for k in range(first, count - 1, 2):
         pairs += [(k, k + 1), (k + 1, k)]
-    return lax.ppermute(a, GX, pairs)
+    return lax.ppermute(a, axis, pairs)
 
 
 def spread(rows, axes):
@@ -475,44 +499,43 @@
 
 def on_device(right_side, diagonal):
     nx, ny, nz = right_side.shape
-    rows = ny + 16
+    rows = ny + 2 * TOP
     shape = lambda *dims: pltpu.VMEM(dims, F32)
-    field = shape(nx + 6, rows, nz)
+    field = shape(2, nx + 6, rows, 128)
     y_face = shape((nx // 2 + nx // 4) * 3 // 2, 8, 128)
     x_face = shape(5 * (ny // 8 + ny // 16) + 5, 8, 128)
     right_side, diagonal = (pltpu.with_memory_space_constraint(a, pltpu.HBM) for a in (right_side, diagonal))
-    yf, yb = call(
+    y_one, y_two = call(
         pack_y,
         "pack_y",
         (y_face, y_face),
         (IN_HBM, IN_HBM),
         scratch=(pltpu.VMEM((4, nx, 8, nz), F32), pltpu.SemaphoreType.DMA((4,))),
     )(right_side, diagonal)
-    ylow = shifted(yf, "z", 1)
-    yhigh = shifted(yb, "z", -1)
+    got_one = swapped(y_one, "z", 0)
+    got_two = swapped(y_two, "z", 1)
     u0, dx, off, on = call(
         load,
         "load",
         (field, field, x_face, x_face),
         (IN_HBM, IN_HBM, IN_VMEM),
-        scratch=(pltpu.SemaphoreType.DMA((2,)),),
+        scratch=(pltpu.VMEM((2, nx, ny, nz), F32), pltpu.SemaphoreType.DMA((2,))),
         flops=10_000_000,
-    )(right_side, diagonal, yf)
+    )(right_side, diagonal, y_one)
     u0, dx, off, on = call(
         corners,
         "corners",
         (field, field, x_face, x_face),
         (IN_VMEM,) * 6,
         aliases={k: k for k in range(4)},
-    )(u0, dx, off, on, ylow, yhigh)
-    off = swapped(off, 1)
-    on = swapped(on, 0)
+    )(u0, dx, off, on, got_one, got_two)
+    off = swapped(off, GX, 1)
+    on = swapped(on, GX, 0)
     u1, u2, u3, sums, shift = call(
         middle,
         "middle",
-        (field, field, shape(nx, ny, nz), shape(6, 8, nz), shape(8, 128)),
+        (field, field, shape(2, nx, ny, 128), shape(6, 8, 128), shape(8, 128)),
         (IN_VMEM,) * 2,
-        scratch=(pltpu.VMEM((rows, nz), F32),),
         flops=20_000_000,
     )(u0, dx)
     up = lambda n: -(-n // 8) * 8
@@ -521,7 +544,7 @@
     u0, dx, u1, u2, u3, line = call(
         rim,
         "rim",
-        (field, field, field, field, shape(nx, ny, nz), shape(up(one), 128)),
+        (field, field, field, field, shape(2, nx, ny, 128), shape(up(one), 128)),
         (IN_VMEM,) * 9,
         aliases={k: k for k in range(5)},
     )(u0, dx, u1, u2, u3, sums, shift, off, on)

time: 68.9 us -> 68.2 us (0.990)
  starting transfers between devices: 19.1 us -> 18.2 us
    ppermute x4, starting transfers between devices: 19.1 us -> 18.2 us  [swapped(): return lax.ppermute(a, axis, pairs)]
where the time goes in v5:
time: 68.2 us; the launch traced here: 67.9 us
  blocking collectives  38.7 us (57%)
  starting transfers between devices  18.2 us (27%)
  Pallas kernels  10.3 us (15%)
  between operations  0.72 us (1%)
    all_to_all x2, blocking collectives, spread(): lax.all_to_all(rows[:count].reshape(count, 1, 128), axes, 0, 0, tiled=True)  38.7 us
    ppermute x4, starting transfers between devices, swapped(): return lax.ppermute(a, axis, pairs)  18.2 us
    pallas_call x1, Pallas kernels, on_device(): call(middle, 'middle', (field, field, shape(2, nx, ny, 128), shape(6, 8,...  3.56 us
    pallas_call x1, Pallas kernels, on_device(): call(load, 'load', (field, field, x_face, x_face), (IN_HBM, IN_HBM, IN_VM...  1.76 us
    pallas_call x1, Pallas kernels, on_device(): call(finish, 'finish', (whole, whole), (IN_VMEM,) * 6, scratch=(pltpu.VME...  1.76 us
    pallas_call x1, Pallas kernels, on_device(): call(rim, 'rim', (field, field, field, field, shape(2, nx, ny, 128), shap...  1.71 us
  transfers between devices with their start and end apart: 4, of which 0 were waited for; matrix products, arithmetic and copies ran while one was open for 0% of the time, Pallas kernels for 8%

profile of v5, /device:TPU:1, one launch (start us, length us, event | category | flops | bytes accessed | tf_op | source)
XLA Modules:
  0.0 67.9 jit_solution(2367416776966945259)
XLA Ops:
  0.6 1.2 %pack_y.1 = (f32[18,8,128]{2,1,0:T(8,128)S(1)}, f32[18,8,128]{2,1,0:T(8,128)S(1)}) custom-call(f32[16,64,192]{2,1,0:T(8,128)} %b.3, f32[16,64,192]{2,1,0:T(8,128)} %d.3), custom_call_target="tpu_custom_call" | custom-call | tf_op jit(solution)/shard_map/pack_y/pallas_call | solution.py:508
  1.9 0.7 collective-permute-start.1
  2.5 8.2 %collective-permute-start = (f32[18,8,128]{2,1,0:T(8,128)S(1)}, f32[18,8,128]{2,1,0:T(8,128)S(1)}, u32[]{:S(2)}, u32[]{:S(2)}) collective-permute-start(f32[18,8,128]{2,1,0:T(8,128)S(1)} %get-tuple-element.22.face), channel_id=1, source_target_pairs={{0,1},{1,0},{2,3},{3,2},{4,5},{5,4},{6,7},{7,6},{8,9},{9,8},{10,11... | collective-permute-start | bytes 221192 | tf_op jit(solution)/shard_map/ppermute | solution.py:473
  10.7 1.8 %load.1 = (f32[2,22,96,128]{3,2,1,0:T(8,128)S(1)}, f32[2,22,96,128]{3,2,1,0:T(8,128)S(1)}, f32[65,8,128]{2,1,0:T(8,128)S(1)}, f32[65,8,128]{2,1,0:T(8,128)S(1)}) custom-call(f32[16,64,192]{2,1,0:T(8,128)} %b.3, f32[16,64,192]{2,1,0:T(8,128)} %d.3, f32[18,8,128]{2,1,0:T(8,128)S(1)} %get-tuple-element.22.face), custom_call_target="tpu_custom_call" | custom-call | flops 10000000 | tf_op jit(solution)/shard_map/load/pallas_call | solution.py:517
  12.5 0.0 collective-permute-done.1.got_two
  12.5 0.0 collective-permute-done.got_one
  12.5 0.2 corners.1
  12.7 4.7 %collective-permute-start.2 = (f32[65,8,128]{2,1,0:T(8,128)S(1)}, f32[65,8,128]{2,1,0:T(8,128)S(1)}, u32[]{:S(2)}, u32[]{:S(2)}) collective-permute-start(f32[65,8,128]{2,1,0:T(8,128)S(1)} %get-tuple-element.35), channel_id=1, source_target_pairs={{12,24},{24,12},{36,48},{48,36},{60,72},{72,60},{84,96},{96,84},{1... | collective-permute-start | bytes 798728 | tf_op jit(solution)/shard_map/ppermute | solution.py:473
  17.4 4.6 %collective-permute-start.3 = (f32[65,8,128]{2,1,0:T(8,128)S(1)}, f32[65,8,128]{2,1,0:T(8,128)S(1)}, u32[]{:S(2)}, u32[]{:S(2)}) collective-permute-start(f32[65,8,128]{2,1,0:T(8,128)S(1)} %get-tuple-element.36), channel_id=1, source_target_pairs={{0,12},{12,0},{24,36},{36,24},{48,60},{60,48},{72,84},{84,72},{96,... | collective-permute-start | bytes 798728 | tf_op jit(solution)/shard_map/ppermute | solution.py:473
  22.0 3.6 %middle.1 = (f32[2,22,96,128]{3,2,1,0:T(8,128)S(1)}, f32[2,22,96,128]{3,2,1,0:T(8,128)S(1)}, f32[2,16,64,128]{3,2,1,0:T(8,128)S(1)}, f32[6,8,128]{2,1,0:T(8,128)S(1)}, f32[8,128]{1,0:T(8,128)S(1)}) custom-call(f32[2,22,96,128]{3,2,1,0:T(8,128)S(1)} %get-tuple-element.28.u0.u0_in, f32[2,22,96,128]{3,2,1,0:T(8,128)S(1)} %get-tuple-element.29.dx.dx_in), custom_call_target="tpu_custom_call" | custom-call | flops 20000000 | tf_op jit(solution)/shard_map/middle/pallas_call | solution.py:534
  25.6 0.0 collective-permute-done.2.off
  25.6 0.0 collective-permute-done.3.on
  25.6 1.7 %rim.1 = (f32[2,22,96,128]{3,2,1,0:T(8,128)S(1)}, f32[2,22,96,128]{3,2,1,0:T(8,128)S(1)}, f32[2,22,96,128]{3,2,1,0:T(8,128)S(1)}, f32[2,22,96,128]{3,2,1,0:T(8,1...) custom-call(f32[2,22,96,128]{3,2,1,0:T(8,128)S(1)} %get-tuple-elemen, ...), custom_call_target="tpu_custom_call", output_to_operand_aliasing={{0}: (0, {}), {1}: (1, {}), {2}: (2, {}), {3}: (3, {}), {4}... | custom-call | tf_op jit(solution)/shard_map/rim/pallas_call | solution.py:544
  27.3 20.9 %all_to_all.10 = f32[24,1,128]{2,1,0:T(1,128)S(1)} all-to-all(f32[24,1,128]{2,1,0:T(1,128)S(1)} %bitcast.11), channel_id=1, replica_groups=mesh['y'=8,'x'=4,'c'=2,'z'=12] {'c','z'}, dimensions={0} | all-to-all | bytes 24576 | tf_op jit(solution)/shard_map/all_to_all | solution.py:478
  48.2 0.1 regroup.1
  48.3 17.8 %all_to_all.11 = f32[32,1,128]{2,1,0:T(1,128)S(1)} all-to-all(f32[32,1,128]{2,1,0:T(1,128)S(1)} %bitcast.9), channel_id=1, replica_groups=mesh['y'=8,'x'=4,'c'=2,'z'=12] {'y','x'}, dimensions={0} | all-to-all | bytes 32768 | tf_op jit(solution)/shard_map/all_to_all | solution.py:478
  66.1 1.8 %finish.1 = (f32[16,64,192]{2,1,0:T(8,128)}, f32[16,64,192]{2,1,0:T(8,128)}) custom-call(f32[32,128]{1,0:T(8,128)S(1)} %bitcast.8, f32[8,128]{1,0:T(8,128)S(1)} %get-tuple-element.34.shift_in, f32[2,22,96,128]{3,2,1,0:T(8,128)S(1)} %get-tuple-element.38.u0, f32[2,22,96,128]{3,2,1,0:T(8,128)S(1)} %get-tuple-element.39.u1, ...), custom_call_target="tpu_custom_call" | custom-call | tf_op jit(solution)/shard_map/finish/pallas_call | solution.py:555
Async XLA Ops:
  1.9 10.6 %collective-permute-start.1 = (f32[18,8,128]{2,1,0:T(8,128)S(1)}, f32[18,8,128]{2,1,0:T(8,128)S(1)}, u32[]{:S(2)}, u32[]{:S(2)}) collective-permute-start(f32[18,8,128]{2,1,0:T(8,128)S(1)} %get-tuple-element.27), channel_id=1, source_target_pairs={{1,2},{2,1},{3,4},{4,3},{5,6},{6,5},{7,8},{8,7},{9,10},{10,9},{13,... | collective-permute-start | bytes 221192 | tf_op jit(solution)/shard_map/ppermute | solution.py:473
  2.5 9.9 %collective-permute-start = (f32[18,8,128]{2,1,0:T(8,128)S(1)}, f32[18,8,128]{2,1,0:T(8,128)S(1)}, u32[]{:S(2)}, u32[]{:S(2)}) collective-permute-start(f32[18,8,128]{2,1,0:T(8,128)S(1)} %get-tuple-element.22.face), channel_id=1, source_target_pairs={{0,1},{1,0},{2,3},{3,2},{4,5},{5,4},{6,7},{7,6},{8,9},{9,8},{10,11... | collective-permute-start | bytes 221192 | tf_op jit(solution)/shard_map/ppermute | solution.py:473
  12.7 12.9 %collective-permute-start.2 = (f32[65,8,128]{2,1,0:T(8,128)S(1)}, f32[65,8,128]{2,1,0:T(8,128)S(1)}, u32[]{:S(2)}, u32[]{:S(2)}) collective-permute-start(f32[65,8,128]{2,1,0:T(8,128)S(1)} %get-tuple-element.35), channel_id=1, source_target_pairs={{12,24},{24,12},{36,48},{48,36},{60,72},{72,60},{84,96},{96,84},{1... | collective-permute-start | bytes 798728 | tf_op jit(solution)/shard_map/ppermute | solution.py:473
  17.4 8.2 %collective-permute-start.3 = (f32[65,8,128]{2,1,0:T(8,128)S(1)}, f32[65,8,128]{2,1,0:T(8,128)S(1)}, u32[]{:S(2)}, u32[]{:S(2)}) collective-permute-start(f32[65,8,128]{2,1,0:T(8,128)S(1)} %get-tuple-element.36), channel_id=1, source_target_pairs={{0,12},{12,0},{24,36},{36,24},{48,60},{60,48},{72,84},{84,72},{96,... | collective-permute-start | bytes 798728 | tf_op jit(solution)/shard_map/ppermute | solution.py:473

commit v6 on v5

--- a/solution.py
+++ b/solution.py
@@ -125,7 +125,7 @@
     two[...] = jnp.where(even, done[1], done[0])
 
 
-def load(b, d, face, u0, dx, off, on, stage, sems):
+def load(b, d, face, u0, dx, u1, off, on, shift_out, stage, sems):
     where = place()
     nx, ny, _ = b.shape
     copies = [pltpu.make_async_copy(source, stage.at[k], sems.at[k]) for k, source in enumerate((b, d))]
@@ -150,6 +150,31 @@
             out[at : at + own] = into[0, slab, TOP : TOP + ny, :].reshape(own, 8, 128)
             rest = into[1, slab, TOP : TOP + ny, :]
             out[at + own : at + own + own // 2] = (rest[:mid] + half_turn(rest[mid:])).reshape(own // 2, 8, 128)
+    zero = jnp.zeros((8, 128), F32)
+    inner = range(TOP + PART, TOP + ny - PART, PART)
+
+    def probe(i, carry):
+        norm, lift = carry
+        at = 5 + 3 * i
+        for row in inner:
+            for p, new in enumerate(stencil(u0, dx, at, 6.0, row, PART)):
+                mid = u0[p, at, row : row + PART, :]
+                norm = norm + fold(mid * mid)
+                lift = lift + fold(mid * new)
+        return norm, lift
+
+    norm, lift = lax.fori_loop(0, 4, probe, (zero, zero), unroll=2)
+    norm = total(norm)
+    lift = total(lift)
+    shift = jnp.where(norm > 0.0, lift / jnp.where(norm > 0.0, norm, 1.0), SHIFT)
+    shift = to_grain(jnp.clip(shift, 0.0, 14.0))
+    shift_out[...] = shift
+    base = 6.0 - shift[0:1, :]
+    def first(i, carry):
+        raised(u1, u0, dx, i, base, None, rows=inner)
+        return carry
+
+    lax.fori_loop(4, nx + 2, first, 0, unroll=2)
 
 
 def lone(rest, second):
@@ -221,11 +246,13 @@
     return jnp.broadcast_to(jnp.sum(a, axis=(0, 1), keepdims=True), (8, 128))
 
 
-def raised(into, field, dx, at, base, there, factor=None):
+def raised(into, field, dx, at, base, there, factor=None, rows=None):
     ny = field.shape[2] - 2 * TOP
-    for row in range(TOP, TOP + ny, PART):
+    for row in rows or range(TOP, TOP + ny, PART):
         for p, new in enumerate(stencil(field, dx, at, base, row, PART)):
             into[p, at, row : row + PART, :] = new if factor is None else new * factor
+    if there is None:
+        return
     for row, edge in ((TOP - 8, there[0]), (TOP + ny, there[1])):
         edge = edge if factor is None else edge * factor
         for p, new in enumerate(stencil(field, dx, at, base, row, 8)):
@@ -247,33 +274,16 @@
     return tuple(sums)
 
 
-def middle(u0, dx, u1, u2, u3, sums_out, shift_out):
+def middle(u0, dx, u1_in, shift, u1, u2, u3, sums_out):
     where = place()
     nx = u0.shape[1] - 6
     ny = u0.shape[2] - 2 * TOP
     there = [where[k].astype(F32) for k in (3, 4)]
     zero = jnp.zeros((8, 128), F32)
-
-    def probe(i, carry):
-        norm, lift = carry
-        at = 5 + 3 * i
-        for row in range(TOP, TOP + ny, PART):
-            for p, new in enumerate(stencil(u0, dx, at, 6.0, row, PART)):
-                mid = u0[p, at, row : row + PART, :]
-                norm = norm + fold(mid * mid)
-                lift = lift + fold(mid * new)
-        return norm, lift
-
-    norm, lift = lax.fori_loop(0, 4, probe, (zero, zero), unroll=2)
-    norm = total(norm)
-    lift = total(lift)
-    shift = jnp.where(norm > 0.0, lift / jnp.where(norm > 0.0, norm, 1.0), SHIFT)
-    shift = to_grain(jnp.clip(shift, 0.0, 14.0))
-    shift_out[...] = shift
     base = 6.0 - shift[0:1, :]
 
     def first(i, carry):
-        raised(u1, u0, dx, i, base, there)
+        raised(u1, u0, dx, i, base, there, rows=(TOP, TOP + ny - PART))
         return carry
 
     def second(i, carry):
@@ -514,10 +524,10 @@
     )(right_side, diagonal)
     got_one = swapped(y_one, "z", 0)
     got_two = swapped(y_two, "z", 1)
-    u0, dx, off, on = call(
+    u0, dx, u1, off, on, shift = call(
         load,
         "load",
-        (field, field, x_face, x_face),
+        (field, field, field, x_face, x_face, shape(8, 128)),
         (IN_HBM, IN_HBM, IN_VMEM),
         scratch=(pltpu.VMEM((2, nx, ny, nz), F32), pltpu.SemaphoreType.DMA((2,))),
         flops=10_000_000,
@@ -531,13 +541,14 @@
     )(u0, dx, off, on, got_one, got_two)
     off = swapped(off, GX, 1)
     on = swapped(on, GX, 0)
-    u1, u2, u3, sums, shift = call(
+    u1, u2, u3, sums = call(
         middle,
         "middle",
-        (field, field, shape(2, nx, ny, 128), shape(6, 8, 128), shape(8, 128)),
-        (IN_VMEM,) * 2,
+        (field, field, shape(2, nx, ny, 128), shape(6, 8, 128)),
+        (IN_VMEM,) * 4,
+        aliases={2: 0},
         flops=20_000_000,
-    )(u0, dx)
+    )(u0, dx, u1, shift)
     up = lambda n: -(-n // 8) * 8
     one = lax.axis_size(FIRST)
     two = lax.axis_size(SECOND)

time: 68.2 us -> 68.1 us (level)
  starting transfers between devices: 18.2 us -> 17.1 us
    ppermute x4, starting transfers between devices: 18.2 us -> 17.1 us  [swapped(): return lax.ppermute(a, axis, pairs)]
    pallas_call x1, Pallas kernels: 1.76 us -> 2.84 us  [on_device(): call(load, 'load', (field, field, field, x_face, x_face, shape(8, 128)),...]
  transfers between devices with their start and end apart: 4 -> 4, of which waited for: 0 -> 0; matrix products, arithmetic and copies ran while one was open for 0% -> 0% of each run, Pallas kernels for 8% -> 9%
where the time goes in v6:
time: 68.1 us; the launch traced here: 67.7 us
  blocking collectives  39.2 us (58%)
  starting transfers between devices  17.1 us (25%)
  Pallas kernels  10.7 us (16%)
  between operations  0.72 us (1%)
    all_to_all x2, blocking collectives, spread(): lax.all_to_all(rows[:count].reshape(count, 1, 128), axes, 0, 0, tiled=True)  39.2 us
    ppermute x4, starting transfers between devices, swapped(): return lax.ppermute(a, axis, pairs)  17.1 us
    pallas_call x1, Pallas kernels, on_device(): call(middle, 'middle', (field, field, shape(2, nx, ny, 128), shape(6, 8,...  2.93 us
    pallas_call x1, Pallas kernels, on_device(): call(load, 'load', (field, field, field, x_face, x_face, shape(8, 128)),...  2.84 us
    pallas_call x1, Pallas kernels, on_device(): call(finish, 'finish', (whole, whole), (IN_VMEM,) * 6, scratch=(pltpu.VME...  1.76 us
    pallas_call x1, Pallas kernels, on_device(): call(rim, 'rim', (field, field, field, field, shape(2, nx, ny, 128), shap...  1.71 us
  transfers between devices with their start and end apart: 4, of which 0 were waited for; matrix products, arithmetic and copies ran while one was open for 0% of the time, Pallas kernels for 9%

profile of v6, /device:TPU:1, one launch (start us, length us, event | category | flops | bytes accessed | tf_op | source)
XLA Modules:
  0.0 67.7 jit_solution(9687928648013447527)
XLA Ops:
  0.6 1.2 %pack_y.1 = (f32[18,8,128]{2,1,0:T(8,128)S(1)}, f32[18,8,128]{2,1,0:T(8,128)S(1)}) custom-call(f32[16,64,192]{2,1,0:T(8,128)} %b.3, f32[16,64,192]{2,1,0:T(8,128)} %d.3), custom_call_target="tpu_custom_call" | custom-call | tf_op jit(solution)/shard_map/pack_y/pallas_call | solution.py:518
  1.9 0.7 collective-permute-start.1
  2.5 8.2 %collective-permute-start = (f32[18,8,128]{2,1,0:T(8,128)S(1)}, f32[18,8,128]{2,1,0:T(8,128)S(1)}, u32[]{:S(2)}, u32[]{:S(2)}) collective-permute-start(f32[18,8,128]{2,1,0:T(8,128)S(1)} %get-tuple-element.23.face), channel_id=1, source_target_pairs={{0,1},{1,0},{2,3},{3,2},{4,5},{5,4},{6,7},{7,6},{8,9},{9,8},{10,11... | collective-permute-start | bytes 221192 | tf_op jit(solution)/shard_map/ppermute | solution.py:483
  10.7 2.8 %load.1 = (f32[2,22,96,128]{3,2,1,0:T(8,128)S(1)}, f32[2,22,96,128]{3,2,1,0:T(8,128)S(1)}, f32[2,22,96,128]{3,2,1,0:T(8,128)S(1)}, f32[65,8,128]{2,1,0:T(8,128)S...) custom-call(f32[16,64,192]{2,1,0:T(8,128)} %b.3, f32[16,64,192]{2,1,0:T(8,128)} %d.3, ...), custom_call_target="tpu_custom_call" | custom-call | flops 10000000 | tf_op jit(solution)/shard_map/load/pallas_call | solution.py:527
  13.5 0.0 collective-permute-done.1.got_two
  13.6 0.0 collective-permute-done.got_one
  13.6 0.2 corners.1
  13.7 4.2 %collective-permute-start.2 = (f32[65,8,128]{2,1,0:T(8,128)S(1)}, f32[65,8,128]{2,1,0:T(8,128)S(1)}, u32[]{:S(2)}, u32[]{:S(2)}) collective-permute-start(f32[65,8,128]{2,1,0:T(8,128)S(1)} %get-tuple-element.37), channel_id=1, source_target_pairs={{12,24},{24,12},{36,48},{48,36},{60,72},{72,60},{84,96},{96,84},{1... | collective-permute-start | bytes 798728 | tf_op jit(solution)/shard_map/ppermute | solution.py:483
  18.0 4.0 %collective-permute-start.3 = (f32[65,8,128]{2,1,0:T(8,128)S(1)}, f32[65,8,128]{2,1,0:T(8,128)S(1)}, u32[]{:S(2)}, u32[]{:S(2)}) collective-permute-start(f32[65,8,128]{2,1,0:T(8,128)S(1)} %get-tuple-element.38), channel_id=1, source_target_pairs={{0,12},{12,0},{24,36},{36,24},{48,60},{60,48},{72,84},{84,72},{96,... | collective-permute-start | bytes 798728 | tf_op jit(solution)/shard_map/ppermute | solution.py:483
  22.0 2.9 %middle.1 = (f32[2,22,96,128]{3,2,1,0:T(8,128)S(1)}, f32[2,22,96,128]{3,2,1,0:T(8,128)S(1)}, f32[2,16,64,128]{3,2,1,0:T(8,128)S(1)}, f32[6,8,128]{2,1,0:T(8,128)S(1)}) custom-call(f32[2,22,96,128]{3,2,1,0:T(8,128)S(1)} %get-tuple-element.29.u0.u0_in, f32[2,22,96,128]{3,2,1,0:T(8,128)S(1)} %get-tuple-element.30.dx.dx_in, ...), custom_call_target="tpu_custom_call", output_to_operand_aliasing={{0}: (2, {})} | custom-call | flops 20000000 | tf_op jit(solution)/shard_map/middle/pallas_call | solution.py:544
  25.0 0.0 collective-permute-done.2.off
  25.0 0.0 collective-permute-done.3.on
  25.0 1.7 %rim.1 = (f32[2,22,96,128]{3,2,1,0:T(8,128)S(1)}, f32[2,22,96,128]{3,2,1,0:T(8,128)S(1)}, f32[2,22,96,128]{3,2,1,0:T(8,128)S(1)}, f32[2,22,96,128]{3,2,1,0:T(8,1...) custom-call(f32[2,22,96,128]{3,2,1,0:T(8,128)S(1)} %get-tuple-elemen, ...), custom_call_target="tpu_custom_call", output_to_operand_aliasing={{0}: (0, {}), {1}: (1, {}), {2}: (2, {}), {3}: (3, {}), {4}... | custom-call | tf_op jit(solution)/shard_map/rim/pallas_call | solution.py:555
  26.7 20.9 %all_to_all.10 = f32[24,1,128]{2,1,0:T(1,128)S(1)} all-to-all(f32[24,1,128]{2,1,0:T(1,128)S(1)} %bitcast.11), channel_id=1, replica_groups=mesh['y'=8,'x'=4,'c'=2,'z'=12] {'c','z'}, dimensions={0} | all-to-all | bytes 24576 | tf_op jit(solution)/shard_map/all_to_all | solution.py:488
  47.6 0.1 regroup.1
  47.7 18.3 %all_to_all.11 = f32[32,1,128]{2,1,0:T(1,128)S(1)} all-to-all(f32[32,1,128]{2,1,0:T(1,128)S(1)} %bitcast.9), channel_id=1, replica_groups=mesh['y'=8,'x'=4,'c'=2,'z'=12] {'y','x'}, dimensions={0} | all-to-all | bytes 32768 | tf_op jit(solution)/shard_map/all_to_all | solution.py:488
  66.0 1.8 %finish.1 = (f32[16,64,192]{2,1,0:T(8,128)}, f32[16,64,192]{2,1,0:T(8,128)}) custom-call(f32[32,128]{1,0:T(8,128)S(1)} %bitcast.8, f32[8,128]{1,0:T(8,128)S(1)} %get-tuple-element.32.shift.shift_in, f32[2,22,96,128]{3,2,1,0:T(8,128)S(1)} %get-tuple-element.40.u0, f32[2,22,96,128]{3,2,1,0:T(8,128)S(1)} %get-tuple-element.41.u1, ...), custom_call_target="tpu_custom_call" | custom-call | tf_op jit(solution)/shard_map/finish/pallas_call | solution.py:566
Async XLA Ops:
  1.9 11.7 %collective-permute-start.1 = (f32[18,8,128]{2,1,0:T(8,128)S(1)}, f32[18,8,128]{2,1,0:T(8,128)S(1)}, u32[]{:S(2)}, u32[]{:S(2)}) collective-permute-start(f32[18,8,128]{2,1,0:T(8,128)S(1)} %get-tuple-element.28), channel_id=1, source_target_pairs={{1,2},{2,1},{3,4},{4,3},{5,6},{6,5},{7,8},{8,7},{9,10},{10,9},{13,... | collective-permute-start | bytes 221192 | tf_op jit(solution)/shard_map/ppermute | solution.py:483
  2.5 11.0 %collective-permute-start = (f32[18,8,128]{2,1,0:T(8,128)S(1)}, f32[18,8,128]{2,1,0:T(8,128)S(1)}, u32[]{:S(2)}, u32[]{:S(2)}) collective-permute-start(f32[18,8,128]{2,1,0:T(8,128)S(1)} %get-tuple-element.23.face), channel_id=1, source_target_pairs={{0,1},{1,0},{2,3},{3,2},{4,5},{5,4},{6,7},{7,6},{8,9},{9,8},{10,11... | collective-permute-start | bytes 221192 | tf_op jit(solution)/shard_map/ppermute | solution.py:483
  13.7 11.2 %collective-permute-start.2 = (f32[65,8,128]{2,1,0:T(8,128)S(1)}, f32[65,8,128]{2,1,0:T(8,128)S(1)}, u32[]{:S(2)}, u32[]{:S(2)}) collective-permute-start(f32[65,8,128]{2,1,0:T(8,128)S(1)} %get-tuple-element.37), channel_id=1, source_target_pairs={{12,24},{24,12},{36,48},{48,36},{60,72},{72,60},{84,96},{96,84},{1... | collective-permute-start | bytes 798728 | tf_op jit(solution)/shard_map/ppermute | solution.py:483
  18.0 7.0 %collective-permute-start.3 = (f32[65,8,128]{2,1,0:T(8,128)S(1)}, f32[65,8,128]{2,1,0:T(8,128)S(1)}, u32[]{:S(2)}, u32[]{:S(2)}) collective-permute-start(f32[65,8,128]{2,1,0:T(8,128)S(1)} %get-tuple-element.38), channel_id=1, source_target_pairs={{0,12},{12,0},{24,36},{36,24},{48,60},{60,48},{72,84},{84,72},{96,... | collective-permute-start | bytes 798728 | tf_op jit(solution)/shard_map/ppermute | solution.py:483

commit v7 on v6

--- a/solution.py
+++ b/solution.py
@@ -125,17 +125,13 @@
     two[...] = jnp.where(even, done[1], done[0])
 
 
-def load(b, d, face, u0, dx, u1, off, on, shift_out, stage, sems):
+def load(b, d, face, u0, dx, u1, off, on, shift_out):
     where = place()
     nx, ny, _ = b.shape
-    copies = [pltpu.make_async_copy(source, stage.at[k], sems.at[k]) for k, source in enumerate((b, d))]
-    for copy in copies:
-        copy.start()
-    for k, (copy, into) in enumerate(zip(copies, (u0, dx))):
-        copy.wait()
+    for source, into in ((b, u0), (d, dx)):
 
         def one(i, carry):
-            main, rest = lanes(stage[k, i])
+            main, rest = lanes(source[i])
             into[0, i + 3, TOP : TOP + ny, :] = main
             into[1, i + 3, TOP : TOP + ny, :] = rest
             return carry
@@ -514,22 +510,20 @@
     field = shape(2, nx + 6, rows, 128)
     y_face = shape((nx // 2 + nx // 4) * 3 // 2, 8, 128)
     x_face = shape(5 * (ny // 8 + ny // 16) + 5, 8, 128)
-    right_side, diagonal = (pltpu.with_memory_space_constraint(a, pltpu.HBM) for a in (right_side, diagonal))
     y_one, y_two = call(
         pack_y,
         "pack_y",
         (y_face, y_face),
         (IN_HBM, IN_HBM),
         scratch=(pltpu.VMEM((4, nx, 8, nz), F32), pltpu.SemaphoreType.DMA((4,))),
-    )(right_side, diagonal)
+    )(*(pltpu.with_memory_space_constraint(a, pltpu.HBM) for a in (right_side, diagonal)))
     got_one = swapped(y_one, "z", 0)
     got_two = swapped(y_two, "z", 1)
     u0, dx, u1, off, on, shift = call(
         load,
         "load",
         (field, field, field, x_face, x_face, shape(8, 128)),
-        (IN_HBM, IN_HBM, IN_VMEM),
-        scratch=(pltpu.VMEM((2, nx, ny, nz), F32), pltpu.SemaphoreType.DMA((2,))),
+        (IN_VMEM,) * 3,
         flops=10_000_000,
     )(right_side, diagonal, y_one)
     u0, dx, off, on = call(

time: 68.1 us -> 68.2 us (level)
  Pallas kernels: 10.7 us -> 9.4 us
  starting transfers between devices: 17.1 us -> 18.2 us
    pallas_call x1, Pallas kernels: 2.84 us -> 1.38 us  [on_device(): call(load, 'load', (field, field, field, x_face, x_face, shape(8, 128)),...]
    ppermute x4, starting transfers between devices: 17.1 us -> 18.2 us  [swapped(): return lax.ppermute(a, axis, pairs)]
  transfers between devices with their start and end apart: 4 -> 4, of which waited for: 0 -> 1; matrix products, arithmetic and copies ran while one was open for 0% -> 0% of each run, Pallas kernels for 9% -> 6%
where the time goes in v7:
time: 68.2 us; the launch traced here: 67.9 us
  blocking collectives  39.2 us (57%)
  starting transfers between devices  18.2 us (27%)
  Pallas kernels  9.4 us (14%)
  between operations  0.74 us (1%)
    all_to_all x2, blocking collectives, spread(): lax.all_to_all(rows[:count].reshape(count, 1, 128), axes, 0, 0, tiled=True)  39.2 us
    ppermute x4, starting transfers between devices, swapped(): return lax.ppermute(a, axis, pairs)  18.2 us
    pallas_call x1, Pallas kernels, on_device(): call(middle, 'middle', (field, field, shape(2, nx, ny, 128), shape(6, 8,...  2.93 us
    pallas_call x1, Pallas kernels, on_device(): call(finish, 'finish', (whole, whole), (IN_VMEM,) * 6, scratch=(pltpu.VME...  1.76 us
    pallas_call x1, Pallas kernels, on_device(): call(rim, 'rim', (field, field, field, field, shape(2, nx, ny, 128), shap...  1.71 us
    pallas_call x1, Pallas kernels, on_device(): call(load, 'load', (field, field, field, x_face, x_face, shape(8, 128)),...  1.38 us
    pallas_call x1, Pallas kernels, on_device(): call(pack_y, 'pack_y', (y_face, y_face), (IN_HBM, IN_HBM), scratch=(pltpu...  1.37 us
  transfers between devices with their start and end apart: 4, of which 1 were waited for; matrix products, arithmetic and copies ran while one was open for 0% of the time, Pallas kernels for 6%

profile of v7, /device:TPU:1, one launch (start us, length us, event | category | flops | bytes accessed | tf_op | source)
XLA Modules:
  0.0 67.9 jit_solution(908778029114840820)
XLA Ops:
  0.6 0.0 copy-start.1
  0.6 0.0 copy-start
  0.6 1.4 %pack_y.1 = (f32[18,8,128]{2,1,0:T(8,128)S(1)}, f32[18,8,128]{2,1,0:T(8,128)S(1)}) custom-call(f32[16,64,192]{2,1,0:T(8,128)} %b.3, f32[16,64,192]{2,1,0:T(8,128)} %d.3), custom_call_target="tpu_custom_call" | custom-call | tf_op jit(solution)/shard_map/pack_y/pallas_call | solution.py:513
  2.0 0.7 collective-permute-start.1
  2.7 8.2 %collective-permute-start = (f32[18,8,128]{2,1,0:T(8,128)S(1)}, f32[18,8,128]{2,1,0:T(8,128)S(1)}, u32[]{:S(2)}, u32[]{:S(2)}) collective-permute-start(f32[18,8,128]{2,1,0:T(8,128)S(1)} %get-tuple-element.23.face), channel_id=1, source_target_pairs={{0,1},{1,0},{2,3},{3,2},{4,5},{5,4},{6,7},{7,6},{8,9},{9,8},{10,11... | collective-permute-start | bytes 221192 | tf_op jit(solution)/shard_map/ppermute | solution.py:479
  10.9 0.0 copy-done.1
  10.9 0.0 copy-done
  10.9 1.4 %load.1 = (f32[2,22,96,128]{3,2,1,0:T(8,128)S(1)}, f32[2,22,96,128]{3,2,1,0:T(8,128)S(1)}, f32[2,22,96,128]{3,2,1,0:T(8,128)S(1)}, f32[65,8,128]{2,1,0:T(8,128)S...) custom-call(f32[16,64,192]{2,1,0:T(8,128)S(1)} %copy-done, f32[16,64,192]{2,1,0:T(8,128)S(1)} %copy-done.1, ...), custom_call_target="tpu_custom_call" | custom-call | flops 10000000 | tf_op jit(solution)/shard_map/load/pallas_call | solution.py:522
  12.3 0.0 collective-permute-done.1.got_two
  12.3 0.3 collective-permute-done.got_one
  12.6 0.2 corners.1
  12.8 4.8 %collective-permute-start.2 = (f32[65,8,128]{2,1,0:T(8,128)S(1)}, f32[65,8,128]{2,1,0:T(8,128)S(1)}, u32[]{:S(2)}, u32[]{:S(2)}) collective-permute-start(f32[65,8,128]{2,1,0:T(8,128)S(1)} %get-tuple-element.37), channel_id=1, source_target_pairs={{12,24},{24,12},{36,48},{48,36},{60,72},{72,60},{84,96},{96,84},{1... | collective-permute-start | bytes 798728 | tf_op jit(solution)/shard_map/ppermute | solution.py:479
  17.6 4.6 %collective-permute-start.3 = (f32[65,8,128]{2,1,0:T(8,128)S(1)}, f32[65,8,128]{2,1,0:T(8,128)S(1)}, u32[]{:S(2)}, u32[]{:S(2)}) collective-permute-start(f32[65,8,128]{2,1,0:T(8,128)S(1)} %get-tuple-element.38), channel_id=1, source_target_pairs={{0,12},{12,0},{24,36},{36,24},{48,60},{60,48},{72,84},{84,72},{96,... | collective-permute-start | bytes 798728 | tf_op jit(solution)/shard_map/ppermute | solution.py:479
  22.2 2.9 %middle.1 = (f32[2,22,96,128]{3,2,1,0:T(8,128)S(1)}, f32[2,22,96,128]{3,2,1,0:T(8,128)S(1)}, f32[2,16,64,128]{3,2,1,0:T(8,128)S(1)}, f32[6,8,128]{2,1,0:T(8,128)S(1)}) custom-call(f32[2,22,96,128]{3,2,1,0:T(8,128)S(1)} %get-tuple-element.29.u0.u0_in, f32[2,22,96,128]{3,2,1,0:T(8,128)S(1)} %get-tuple-element.30.dx.dx_in, ...), custom_call_target="tpu_custom_call", output_to_operand_aliasing={{0}: (2, {})} | custom-call | flops 20000000 | tf_op jit(solution)/shard_map/middle/pallas_call | solution.py:538
  25.1 0.0 collective-permute-done.2.off
  25.1 0.0 collective-permute-done.3.on
  25.1 1.7 %rim.1 = (f32[2,22,96,128]{3,2,1,0:T(8,128)S(1)}, f32[2,22,96,128]{3,2,1,0:T(8,128)S(1)}, f32[2,22,96,128]{3,2,1,0:T(8,128)S(1)}, f32[2,22,96,128]{3,2,1,0:T(8,1...) custom-call(f32[2,22,96,128]{3,2,1,0:T(8,128)S(1)} %get-tuple-elemen, ...), custom_call_target="tpu_custom_call", output_to_operand_aliasing={{0}: (0, {}), {1}: (1, {}), {2}: (2, {}), {3}: (3, {}), {4}... | custom-call | tf_op jit(solution)/shard_map/rim/pallas_call | solution.py:549
  26.9 20.9 %all_to_all.10 = f32[24,1,128]{2,1,0:T(1,128)S(1)} all-to-all(f32[24,1,128]{2,1,0:T(1,128)S(1)} %bitcast.11), channel_id=1, replica_groups=mesh['y'=8,'x'=4,'c'=2,'z'=12] {'c','z'}, dimensions={0} | all-to-all | bytes 24576 | tf_op jit(solution)/shard_map/all_to_all | solution.py:484
  47.8 0.1 regroup.1
  47.9 18.3 %all_to_all.11 = f32[32,1,128]{2,1,0:T(1,128)S(1)} all-to-all(f32[32,1,128]{2,1,0:T(1,128)S(1)} %bitcast.9), channel_id=1, replica_groups=mesh['y'=8,'x'=4,'c'=2,'z'=12] {'y','x'}, dimensions={0} | all-to-all | bytes 32768 | tf_op jit(solution)/shard_map/all_to_all | solution.py:484
  66.1 1.8 %finish.1 = (f32[16,64,192]{2,1,0:T(8,128)}, f32[16,64,192]{2,1,0:T(8,128)}) custom-call(f32[32,128]{1,0:T(8,128)S(1)} %bitcast.8, f32[8,128]{1,0:T(8,128)S(1)} %get-tuple-element.32.shift.shift_in, f32[2,22,96,128]{3,2,1,0:T(8,128)S(1)} %get-tuple-element.40.u0, f32[2,22,96,128]{3,2,1,0:T(8,128)S(1)} %get-tuple-element.41.u1, ...), custom_call_target="tpu_custom_call" | custom-call | tf_op jit(solution)/shard_map/finish/pallas_call | solution.py:560
Async XLA Ops:
  0.6 10.2 %copy-start.1 = (f32[16,64,192]{2,1,0:T(8,128)S(1)}, f32[16,64,192]{2,1,0:T(8,128)}, u32[]{:S(2)}) copy-start(f32[16,64,192]{2,1,0:T(8,128)} %d.3) | copy-start | bytes 2359300
  0.6 10.2 %copy-start = (f32[16,64,192]{2,1,0:T(8,128)S(1)}, f32[16,64,192]{2,1,0:T(8,128)}, u32[]{:S(2)}) copy-start(f32[16,64,192]{2,1,0:T(8,128)} %b.3) | copy-start | bytes 2359300
  2.0 10.2 %collective-permute-start.1 = (f32[18,8,128]{2,1,0:T(8,128)S(1)}, f32[18,8,128]{2,1,0:T(8,128)S(1)}, u32[]{:S(2)}, u32[]{:S(2)}) collective-permute-start(f32[18,8,128]{2,1,0:T(8,128)S(1)} %get-tuple-element.28), channel_id=1, source_target_pairs={{1,2},{2,1},{3,4},{4,3},{5,6},{6,5},{7,8},{8,7},{9,10},{10,9},{13,... | collective-permute-start | bytes 221192 | tf_op jit(solution)/shard_map/ppermute | solution.py:479
  2.7 9.9 %collective-permute-start = (f32[18,8,128]{2,1,0:T(8,128)S(1)}, f32[18,8,128]{2,1,0:T(8,128)S(1)}, u32[]{:S(2)}, u32[]{:S(2)}) collective-permute-start(f32[18,8,128]{2,1,0:T(8,128)S(1)} %get-tuple-element.23.face), channel_id=1, source_target_pairs={{0,1},{1,0},{2,3},{3,2},{4,5},{5,4},{6,7},{7,6},{8,9},{9,8},{10,11... | collective-permute-start | bytes 221192 | tf_op jit(solution)/shard_map/ppermute | solution.py:479
  12.8 12.4 %collective-permute-start.2 = (f32[65,8,128]{2,1,0:T(8,128)S(1)}, f32[65,8,128]{2,1,0:T(8,128)S(1)}, u32[]{:S(2)}, u32[]{:S(2)}) collective-permute-start(f32[65,8,128]{2,1,0:T(8,128)S(1)} %get-tuple-element.37), channel_id=1, source_target_pairs={{12,24},{24,12},{36,48},{48,36},{60,72},{72,60},{84,96},{96,84},{1... | collective-permute-start | bytes 798728 | tf_op jit(solution)/shard_map/ppermute | solution.py:479
  17.6 7.5 %collective-permute-start.3 = (f32[65,8,128]{2,1,0:T(8,128)S(1)}, f32[65,8,128]{2,1,0:T(8,128)S(1)}, u32[]{:S(2)}, u32[]{:S(2)}) collective-permute-start(f32[65,8,128]{2,1,0:T(8,128)S(1)} %get-tuple-element.38), channel_id=1, source_target_pairs={{0,12},{12,0},{24,36},{36,24},{48,60},{60,48},{72,84},{84,72},{96,... | collective-permute-start | bytes 798728 | tf_op jit(solution)/shard_map/ppermute | solution.py:479
